TPU v7x, 256 devices: a whole 4x4x8 slice. The times are simulated.
256 devices in a mesh: seq: 64 (over x, z_lo, y), chan: 4 (over z_hi, core).
Axes of the slice: x: 4, y: 4, z: 8 (z_hi: 2, z_lo: 4; z = z_hi * 4 + z_lo), core: 2. Of those that a mesh axis runs over, the one named last changes fastest.
Arguments:
- fwd_q: bfloat16 [8192, 4096], P('seq', 'chan'), may hold values from -6 to 6
- fwd_k: bfloat16 [8192, 4096], P('seq', 'chan'), may hold values from -6 to 6
- fwd_v: bfloat16 [8192, 4096], P('seq', 'chan'), may hold values from -6 to 6
- bwd_q: bfloat16 [8192, 4096], P('seq', 'chan'), may hold values from -6 to 6
- bwd_k: bfloat16 [8192, 4096], P('seq', 'chan'), may hold values from -6 to 6
- bwd_v: bfloat16 [8192, 4096], P('seq', 'chan'), may hold values from -6 to 6
- bwd_grad: bfloat16 [8192, 4096], P('seq', 'chan'), may hold values from -6 to 6
- filters: float32 [8192, 1024], P('seq', 'chan'), may hold values from -0.0625 to 0.0625
- skip: float32 [4096], P('chan'), may hold values from -4 to 4
Outputs:
- output: bfloat16 [8192, 4096], P('seq', 'chan')
- grad_query: bfloat16 [8192, 4096], P('seq', 'chan')
- grad_key: bfloat16 [8192, 4096], P('seq', 'chan')
- grad_value: bfloat16 [8192, 4096], P('seq', 'chan')
- grad_filter: float32 [8192, 1024], P('seq', 'chan')
- grad_skip: float32 [4096], P('chan')
All inputs are finite; a program needn't handle non-finite values.
Results may differ from a plain program's by a relative error of at most 0.0075.
Values may be sent and summed in bfloat16 or wider, within the bound.
A program may use at most 256 MiB of HBM per device.

v0:
```python
import math

import jax
import jax.numpy as jnp
from jax import lax
from jax.sharding import PartitionSpec as P

HIGHEST = lax.Precision.HIGHEST


def in_order(parts, dim):
    lengths = list(parts.shape[1:])
    lengths[dim] *= parts.shape[0]
    return jnp.moveaxis(parts, 0, dim).reshape(lengths)


def from_everyone(value, axis):
    copies = jnp.broadcast_to(value, (lax.axis_size(axis), *value.shape))
    return lax.all_to_all(copies, axis, split_axis=0, concat_axis=0, tiled=True)


def collect(value, axis, dim):
    return in_order(from_everyone(value, axis), dim)


def shortened(value):
    return jax.tree.map(lambda a: a.astype(jnp.bfloat16) if a.dtype == jnp.float32 else a, value)


def split_up(value, dim, length):
    before, after = (value.shape[:dim], value.shape[dim + 1 :])
    return jnp.moveaxis(value.reshape(*before, length, -1, *after), dim, 0)


def summed_on_arrival(value, axis, dim):
    length = lax.axis_size(axis)
    parts = lax.all_to_all(split_up(value, dim, length), axis, 0, 0, tiled=True)
    return jnp.sum(parts.astype(jnp.float32), axis=0)


def over_copies(value, axis):
    return from_everyone(value, axis).sum(axis=0)


def index_ramp(total):
    return jnp.arange(total, dtype=jnp.int32)


def widened(values):
    return values.astype(jnp.float32)


def angles(out_index, in_index, period, sign):
    phase_steps = out_index[:, None] * in_index[None, :] % period
    phase = phase_steps.astype(jnp.float32) * (sign * 2.0 * math.pi / period)
    return (jnp.cos(phase), jnp.sin(phase))


def times_table(left, right):
    return (left[0] * right[0] - left[1] * right[1], left[0] * right[1] + left[1] * right[0])


def block_table(pair):
    cosine, sine_part = pair
    return jnp.stack([jnp.stack([cosine, -sine_part]), jnp.stack([sine_part, cosine])])


def product_of(left, right):
    return jnp.stack(
        [left[0] * right[0] - left[1] * right[1], left[0] * right[1] + left[1] * right[0]]
    )


def conj_product(left, right):
    return jnp.stack(
        [left[0] * right[0] + left[1] * right[1], left[0] * right[1] - left[1] * right[0]]
    )


def joined(left, right):
    return jnp.concatenate([left, right], axis=-1)


def factor(total):
    chosen = 1
    for candidate in range(1, total + 1):
        if candidate * candidate <= total and total % candidate == 0:
            chosen = candidate
    return chosen


def leading_section(values, seq_size):
    cosine, sine_part = angles(index_ramp(2 * seq_size), index_ramp(seq_size), 2 * seq_size, -1.0)
    table = jnp.stack([cosine, sine_part])
    return jnp.einsum("rkp,pmc->rkmc", table, values, precision=HIGHEST)


def trailing_section(values, seq_size, period):
    cosine, sine_part = angles(index_ramp(seq_size), index_ramp(2 * seq_size), 2 * seq_size, 1.0)
    table = jnp.stack([cosine, -sine_part]) * (1.0 / period)
    return jnp.einsum("rpk,rkmc->pmc", table, values, precision=HIGHEST)


def inner_forward(values, freq_keys, period):
    lead_size, row_count, chan_count = values.shape[1:]
    outer_size = factor(row_count)
    inner_size = row_count // outer_size
    values = values.reshape(2, lead_size, outer_size, inner_size, chan_count)
    first_twiddle = angles(freq_keys, index_ramp(row_count), period, -1.0)
    first_twiddle = tuple(
        (part.reshape(lead_size, outer_size, inner_size) for part in first_twiddle)
    )
    outer_dft = angles(index_ramp(outer_size), index_ramp(outer_size), outer_size, -1.0)
    outer_table = times_table(
        tuple((part[None, :, :, None] for part in outer_dft)),
        tuple((part[:, None, :, :] for part in first_twiddle)),
    )
    values = jnp.einsum("rsjxab,sjabc->rjxbc", block_table(outer_table), values, precision=HIGHEST)
    second_twiddle = angles(index_ramp(outer_size), index_ramp(inner_size), row_count, -1.0)
    inner_dft = angles(index_ramp(inner_size), index_ramp(inner_size), inner_size, -1.0)
    inner_table = times_table(
        tuple((part[None, :, :] for part in inner_dft)),
        tuple((part[:, None, :] for part in second_twiddle)),
    )
    return jnp.einsum("rsxyb,sjxbc->rjxyc", block_table(inner_table), values, precision=HIGHEST)


def inner_inverse(values, freq_keys, period):
    lead_size, outer_size, inner_size, chan_count = values.shape[1:]
    row_count = outer_size * inner_size
    second_twiddle = angles(index_ramp(outer_size), index_ramp(inner_size), row_count, 1.0)
    inner_dft = angles(index_ramp(inner_size), index_ramp(inner_size), inner_size, 1.0)
    inner_table = times_table(
        tuple((part[:, :, None] for part in second_twiddle)),
        tuple((part[None, :, :] for part in inner_dft)),
    )
    values = jnp.einsum("rsxby,sjxyc->rjxbc", block_table(inner_table), values, precision=HIGHEST)
    first_twiddle = angles(freq_keys, index_ramp(row_count), period, 1.0)
    first_twiddle = tuple(
        (part.reshape(lead_size, outer_size, inner_size) for part in first_twiddle)
    )
    outer_dft = angles(index_ramp(outer_size), index_ramp(outer_size), outer_size, 1.0)
    outer_table = times_table(
        tuple((part[:, :, :, None] for part in first_twiddle)),
        tuple((part[None, :, None, :] for part in outer_dft)),
    )
    values = jnp.einsum("rsjabx,sjxbc->rjabc", block_table(outer_table), values, precision=HIGHEST)
    return values.reshape(2, lead_size, row_count, chan_count)


def forward_local(signal_part, seq_size):
    seq_length, chan_count = signal_part.shape
    row_count = seq_length // seq_size
    values = leading_section(signal_part.reshape(seq_size, row_count, chan_count), seq_size)
    return inner_forward(values, index_ramp(2 * seq_size), 2 * seq_length)


def inverse_local(values, seq_size):
    lead_size, outer_size, inner_size, chan_count = values.shape[1:]
    row_count = outer_size * inner_size
    period = 2 * seq_size * row_count
    values = inner_inverse(values, index_ramp(2 * seq_size), period)
    return trailing_section(values, seq_size, period).reshape(seq_size * row_count, chan_count)


def filter_times_pair(spec_filter, spec_pair):
    shape_pair = spec_pair.shape
    width = spec_filter.shape[-1]
    pair_view = spec_pair.reshape(shape_pair[:-1] + (2, width))
    filter_view = spec_filter[..., None, :]
    return product_of(filter_view, pair_view).reshape(shape_pair)


def per_device(fwd_q, fwd_k, fwd_v, bwd_q, bwd_k, bwd_v, bwd_grad, filters, skip):
    row_count, chan_width = fwd_q.shape
    seq_size = lax.axis_size("seq")
    grad_scale = 1.0 / math.sqrt(row_count * seq_size)
    source = (widened(fwd_k) * widened(fwd_v)).astype(jnp.bfloat16)
    second_source = (widened(bwd_k) * widened(bwd_v)).astype(jnp.bfloat16)
    upstream = (widened(bwd_grad) * widened(bwd_q)).astype(jnp.bfloat16)
    skip_gain = widened(skip)
    filters_all = collect(filters, "chan", 1)
    narrow = chan_width // seq_size
    local_first, local_second = (
        lax.all_to_all(source, "seq", split_axis=1, concat_axis=0, tiled=True),
        lax.all_to_all(second_source, "seq", split_axis=1, concat_axis=0, tiled=True),
    )
    local_filter = lax.all_to_all(
        filters_all.astype(jnp.bfloat16), "seq", split_axis=1, concat_axis=0, tiled=True
    ).astype(filters_all.dtype)
    local_up = lax.all_to_all(upstream, "seq", split_axis=1, concat_axis=0, tiled=True)
    spec_sources = forward_local(
        widened(jnp.concatenate([local_first, local_second], axis=1)), seq_size
    )
    spec_filter = forward_local(local_filter, seq_size)
    conv_local = inverse_local(filter_times_pair(spec_filter, spec_sources), seq_size)
    conv_first, conv_second = (
        lax.all_to_all(
            shortened(conv_local[:, :narrow]), "seq", split_axis=0, concat_axis=1, tiled=True
        ),
        lax.all_to_all(
            shortened(conv_local[:, narrow:]), "seq", split_axis=0, concat_axis=1, tiled=True
        ),
    )
    spec_up = forward_local(widened(local_up), seq_size)
    spec_second = spec_sources[..., narrow:]
    back_local = inverse_local(
        joined(conj_product(spec_filter, spec_up), conj_product(spec_second, spec_up)), seq_size
    )
    through_conv, filter_terms = (
        lax.all_to_all(
            shortened(back_local[:, :narrow]), "seq", split_axis=0, concat_axis=1, tiled=True
        ),
        lax.all_to_all(
            shortened(back_local[:, narrow:] * grad_scale),
            "seq",
            split_axis=0,
            concat_axis=1,
            tiled=True,
        ),
    )
    grad_filter = summed_on_arrival(filter_terms.astype(jnp.bfloat16), "chan", 1)
    source_wide = widened(source)
    second_wide = widened(second_source)
    upstream_wide = widened(upstream)
    mixed = conv_first + skip_gain * source_wide
    output = (widened(fwd_q) * mixed).astype(jnp.bfloat16)
    mixed_two = conv_second + skip_gain * second_wide
    grad_query = (widened(bwd_grad) * mixed_two).astype(jnp.bfloat16)
    through = through_conv + skip_gain * upstream_wide
    grad_key = (through * widened(bwd_v)).astype(jnp.bfloat16)
    grad_value = (through * widened(bwd_k)).astype(jnp.bfloat16)
    grad_skip = over_copies(jnp.sum(upstream_wide * second_wide, axis=0) * grad_scale, "seq")
    return (output, grad_query, grad_key, grad_value, grad_filter, grad_skip)


def solution(mesh):
    return jax.shard_map(
        per_device,
        mesh=mesh,
        in_specs=(
            P("seq", "chan"),
            P("seq", "chan"),
            P("seq", "chan"),
            P("seq", "chan"),
            P("seq", "chan"),
            P("seq", "chan"),
            P("seq", "chan"),
            P("seq", "chan"),
            P("chan"),
        ),
        out_specs=(
            P("seq", "chan"),
            P("seq", "chan"),
            P("seq", "chan"),
            P("seq", "chan"),
            P("seq", "chan"),
            P("chan"),
        ),
        check_vma=False,
    )
```

profile of v0, /device:TPU:1, one launch (start us, length us, event | category | flops | bytes accessed | tf_op | source)
XLA Modules:
  0.0 597.7 jit_solution(2515439832459527980)
XLA Ops:
  2.4 9.9 %all-to-all-start = ((bf16[4,128,256]{1,2,0:T(8,128)(2,1)}), bf16[4,128,256]{1,2,0:T(8,128)(2,1)}, u32[]{:S(2)}, u32[]{:S(2)}) async-start(bf16[4,128,256]{1,2,0:T(8,128)(2,1)} %broadcast_in_dim.4), calls=%async_computation | async-start | bytes 524288 | tf_op jit(solution)/shard_map/all_to_all | solution.py:19
  69.7 25.9 %copy.159 = f32[2,2,128,8,8,16]{4,3,1,0,5,2:T(8,128)} copy(f32[2,2,128,8,8,16]{2,5,4,3,1,0:T(8,128)S(1)} %pad_maximum_fusion) | data formatting | bytes 4194304 | tf_op jit(solution)/shard_map/stack | solution.py:65
  95.6 26.1 %copy.172 = f32[2,2,128,8,16,8]{5,3,1,0,4,2:T(8,128)} copy(f32[2,2,128,8,16,8]{2,5,4,3,1,0:T(8,128)} %pad_maximum_fusion.1) | data formatting | bytes 4194304 | tf_op jit(solution)/shard_map/stack | solution.py:65
  124.7 13.5 %copy.211 = f32[2,128,8,16,16,1]{4,2,0,5,3,1:T(8,128)} copy(f32[2,128,8,16,16,1]{1,4,3,2,0,5:T(8,128)S(1)} %convolution_bitcast_fusion.8) | data formatting | bytes 4194304 | tf_op jit(solution)/shard_map/rkp,pmc->rkmc/dot_general | solution.py:95
  138.2 10.8 %all-to-all-start.1 = ((bf16[128,64,16]{0,2,1:T(8,128)(2,1)}), bf16[128,64,16]{0,2,1:T(8,128)(2,1)S(1)}, u32[]{:S(2)}, u32[]{:S(2)}) async-start(bf16[128,64,16]{0,2,1:T(8,128)(2,1)} %bitcast.4), calls=%async_computation.1 | async-start | bytes 524288 | tf_op jit(solution)/shard_map/all_to_all | solution.py:188
  155.5 14.4 %copy.201 = f32[2,128,8,16,32,1]{4,2,0,5,3,1:T(8,128)} copy(f32[2,128,8,16,32,1]{1,4,3,2,0,5:T(8,128)} %convolution_bitcast_fusion.6) | data formatting | bytes 8388608 | tf_op jit(solution)/shard_map/rkp,pmc->rkmc/dot_general | solution.py:95
  169.8 35.4 %convolution_bitcast_fusion.1 = f32[2,128,8,16,16,1]{4,2,0,3,1,5:T(8,128)} fusion(f32[2,128,8,16,16,1]{4,2,0,5,3,1:T(8,128)} %copy.211, f32[2,2,128,8,8,16]{4,3,1,0,5,2:T(8,128)} %copy.159), kind=kOutput, calls=%fused_computation.1 | convolution fusion | flops 100663296 | bytes 6291456 | tf_op jit(solution)/shard_map/rsjxab,sjabc->rjxbc/dot_general | solution.py:118
  205.2 35.4 %convolution_bitcast_fusion.3 = f32[2,128,8,16,32,1]{4,2,0,3,1,5:T(8,128)} fusion(f32[2,128,8,16,32,1]{4,2,0,5,3,1:T(8,128)} %copy.201, f32[2,2,128,8,8,16]{4,3,1,0,5,2:T(8,128)} %copy.159), kind=kOutput, calls=%fused_computation.3 | convolution fusion | flops 201326592 | bytes 10485760 | tf_op jit(solution)/shard_map/rsjxab,sjabc->rjxbc/dot_general | solution.py:118
  240.6 11.0 %copy.213 = f32[2,128,8,16,16,1]{1,3,0,5,4,2:T(8,128)S(1)} copy(f32[2,128,8,16,16,1]{4,2,0,3,1,5:T(8,128)} %convolution_bitcast_fusion.1) | data formatting | bytes 4194304 | tf_op jit(solution)/shard_map/rsjxab,sjabc->rjxbc/transpose | solution.py:118
  251.6 13.0 %copy.203 = f32[2,128,8,16,32,1]{1,3,0,5,4,2:T(8,128)} copy(f32[2,128,8,16,32,1]{4,2,0,3,1,5:T(8,128)} %convolution_bitcast_fusion.3) | data formatting | bytes 8388608 | tf_op jit(solution)/shard_map/rsjxab,sjabc->rjxbc/transpose | solution.py:118
  273.9 10.7 %all-to-all-start.10 = ((f32[64,1,1024]{2,1,0:T(1,128)}), f32[64,1,1024]{2,1,0:T(1,128)S(1)}, u32[]{:S(2)}, u32[]{:S(2)}) async-start(f32[64,1,1024]{2,1,0:T(1,128)} %broadcast_in_dim.5), calls=%async_computation.10 | async-start | bytes 524288 | tf_op jit(solution)/shard_map/all_to_all | solution.py:19
  286.9 13.5 %copy.196 = f32[2,128,8,16,16,1]{4,2,0,5,3,1:T(8,128)} copy(f32[2,128,8,16,16,1]{1,4,3,2,0,5:T(8,128)S(1)} %convolution_bitcast_fusion.10) | data formatting | bytes 4194304 | tf_op jit(solution)/shard_map/rkp,pmc->rkmc/dot_general | solution.py:95
  300.3 35.2 %convolution_bitcast_fusion.4 = f32[2,128,8,16,16,1]{4,2,0,3,1,5:T(8,128)} fusion(f32[2,128,8,16,16,1]{4,2,0,5,3,1:T(8,128)} %copy.196, f32[2,2,128,8,8,16]{4,3,1,0,5,2:T(8,128)} %copy.159), kind=kOutput, calls=%fused_computation.4 | convolution fusion | flops 100663296 | bytes 6291456 | tf_op jit(solution)/shard_map/rsjxab,sjabc->rjxbc/dot_general | solution.py:118
  335.6 11.2 %copy.198 = f32[2,128,8,16,16,1]{1,3,0,5,4,2:T(8,128)S(1)} copy(f32[2,128,8,16,16,1]{4,2,0,3,1,5:T(8,128)} %convolution_bitcast_fusion.4) | data formatting | bytes 4194304 | tf_op jit(solution)/shard_map/rsjxab,sjabc->rjxbc/transpose | solution.py:118
  356.7 15.2 %copy.217 = f32[2,128,8,16,32,1]{4,2,0,5,3,1:T(8,128)} copy(f32[2,128,8,16,32,1]{1,3,0,4,2,5:T(8,128)} %fusion.14) | data formatting | bytes 8388608 | tf_op jit(solution)/shard_map/rsxby,sjxyc->rjxbc/transpose | solution.py:137
  371.8 35.5 %convolution_bitcast_fusion = f32[2,128,8,16,32]{4,2,0,3,1:T(8,128)} fusion(f32[2,128,8,16,32,1]{4,2,0,5,3,1:T(8,128)} %copy.217, f32[2,2,128,8,16,8]{5,3,1,0,4,2:T(8,128)} %copy.172), kind=kOutput, calls=%fused_computation | convolution fusion | flops 201326592 | bytes 10485760 | tf_op jit(solution)/shard_map/rsjabx,sjxbc->rjabc/dot_general | solution.py:147
  407.3 13.7 %copy.185 = f32[2,128,8,16,32]{1,4,3,2,0:T(8,128)} copy(f32[2,128,8,16,32]{4,2,0,3,1:T(8,128)} %convolution_bitcast_fusion) | data formatting | bytes 8388608 | tf_op jit(solution)/shard_map/rsjabx,sjxbc->rjabc/transpose | solution.py:147
  429.2 15.6 %copy.208 = f32[2,128,8,16,32,1]{4,2,0,5,3,1:T(8,128)} copy(f32[2,128,8,16,32,1]{1,3,0,4,2,5:T(8,128)} %fusion.15) | data formatting | bytes 8388608 | tf_op jit(solution)/shard_map/rsxby,sjxyc->rjxbc/transpose | solution.py:137
  444.8 35.3 %convolution_bitcast_fusion.2 = f32[2,128,8,16,32]{4,2,0,3,1:T(8,128)} fusion(f32[2,128,8,16,32,1]{4,2,0,5,3,1:T(8,128)} %copy.208, f32[2,2,128,8,16,8]{5,3,1,0,4,2:T(8,128)} %copy.172), kind=kOutput, calls=%fused_computation.2 | convolution fusion | flops 201326592 | bytes 10485760 | tf_op jit(solution)/shard_map/rsjabx,sjxbc->rjabc/dot_general | solution.py:147
  488.3 13.7 %copy.173 = f32[2,128,8,16,32]{1,4,3,2,0:T(8,128)} copy(f32[2,128,8,16,32]{4,2,0,3,1:T(8,128)} %convolution_bitcast_fusion.2) | data formatting | bytes 8388608 | tf_op jit(solution)/shard_map/rsjabx,sjxbc->rjabc/transpose | solution.py:147
  502.7 10.2 %all-to-all-start.7 = ((bf16[64,128,16]{1,2,0:T(8,128)(2,1)}), bf16[64,128,16]{1,2,0:T(8,128)(2,1)S(1)}, u32[]{:S(2)}, u32[]{:S(2)}) async-start(bf16[64,128,16]{1,2,0:T(8,128)(2,1)} %copy_bitcast_fusion.3), calls=%async_computation.7 | async-start | bytes 524288 | tf_op jit(solution)/shard_map/all_to_all | solution.py:211
  548.0 10.4 %all-to-all-done.4 = bf16[64,128,16]{1,2,0:T(8,128)(2,1)S(1)} async-done(((bf16[64,128,16]{1,2,0:T(8,128)(2,1)}), bf16[64,128,16]{1,2,0:T(8,128)(2,1)S(1)}, u32[]{:S(2)}, u32[]{:S(2)}) %all-to-all-start.4) | async-done | bytes 262176 | tf_op jit(solution)/shard_map/all_to_all | solution.py:198
  558.4 15.0 %all_to_all.126 = bf16[64,128,16]{1,2,0:T(8,128)(2,1)} all-to-all(bf16[64,128,16]{1,2,0:T(8,128)(2,1)S(1)} %copy_bitcast_fusion.2), channel_id=1, replica_groups=mesh['seq'=64,'chan'=4] {'seq'}, dimensions={0} | all-to-all | bytes 524288 | tf_op jit(solution)/shard_map/all_to_all | solution.py:214
  573.4 14.4 %all-to-all-start.9 = ((bf16[4,128,256]{1,2,0:T(8,128)(2,1)}), bf16[4,128,256]{1,2,0:T(8,128)(2,1)S(1)}, u32[]{:S(2)}, u32[]{:S(2)}) async-start(bf16[4,128,256]{1,2,0:T(8,128)(2,1)} %bitcast.99), calls=%async_computation.9 | async-start | bytes 524288 | tf_op jit(solution)/shard_map/all_to_all | solution.py:37
  (117 shorter events, 151.6 us)
Async XLA Ops:
  2.4 22.7 %all-to-all-start = ((bf16[4,128,256]{1,2,0:T(8,128)(2,1)}), bf16[4,128,256]{1,2,0:T(8,128)(2,1)}, u32[]{:S(2)}, u32[]{:S(2)}) async-start(bf16[4,128,256]{1,2,0:T(8,128)(2,1)} %broadcast_in_dim.4), calls=%async_computation | async-start | bytes 524288 | tf_op jit(solution)/shard_map/all_to_all | solution.py:19
  13.6 9.8 %copy-start.3 = (bf16[128,1024]{0,1:T(8,128)(2,1)}, bf16[128,1024]{0,1:T(8,128)(2,1)S(1)}, u32[]{:S(2)}) copy-start(bf16[128,1024]{0,1:T(8,128)(2,1)S(1)} %copy.164) | copy-start | bytes 786436
  16.0 7.5 %copy-start.5 = (bf16[128,1024]{0,1:T(8,128)(2,1)}, bf16[128,1024]{0,1:T(8,128)(2,1)S(1)}, u32[]{:S(2)}) copy-start(bf16[128,1024]{0,1:T(8,128)(2,1)S(1)} %copy.176) | copy-start | bytes 786436
  17.2 6.2 %copy-start.7 = (bf16[128,1024]{0,1:T(8,128)(2,1)}, bf16[128,1024]{0,1:T(8,128)(2,1)S(1)}, u32[]{:S(2)}) copy-start(bf16[128,1024]{0,1:T(8,128)(2,1)S(1)} %copy.165) | copy-start | bytes 786436
  25.1 20.7 %all-to-all-start.6 = ((bf16[128,64,16]{0,2,1:T(8,128)(2,1)}), bf16[128,64,16]{0,2,1:T(8,128)(2,1)S(1)}, u32[]{:S(2)}, u32[]{:S(2)}) async-start(bf16[128,64,16]{0,2,1:T(8,128)(2,1)} %bitcast.69), calls=%async_computation.6 | async-start | bytes 524288 | tf_op jit(solution)/shard_map/all_to_all | solution.py:191
  45.8 6.0 %copy-start.9 = (bf16[128,64,16]{0,2,1:T(8,128)(2,1)}, bf16[128,64,16]{0,2,1:T(8,128)(2,1)S(1)}, u32[]{:S(2)}) copy-start(bf16[128,64,16]{0,2,1:T(8,128)(2,1)S(1)} %all-to-all-done.6) | copy-start | bytes 786436
  45.8 16.3 %all-to-all-start.3 = ((bf16[128,64,16]{0,2,1:T(8,128)(2,1)}), bf16[128,64,16]{0,2,1:T(8,128)(2,1)}, u32[]{:S(2)}, u32[]{:S(2)}) async-start(bf16[128,64,16]{0,2,1:T(8,128)(2,1)} %bitcast.28), calls=%async_computation.3 | async-start | bytes 524288 | tf_op jit(solution)/shard_map/all_to_all | solution.py:186
  62.1 76.1 %all-to-all-start.2 = ((bf16[128,64,16]{0,2,1:T(8,128)(2,1)}), bf16[128,64,16]{0,2,1:T(8,128)(2,1)S(1)}, u32[]{:S(2)}, u32[]{:S(2)}) async-start(bf16[128,64,16]{0,2,1:T(8,128)(2,1)} %bitcast.26), calls=%async_computation.2 | async-start | bytes 524288 | tf_op jit(solution)/shard_map/all_to_all | solution.py:185
  95.6 26.8 %copy-start.17 = (f32[1024]{0:T(1024)S(1)}, f32[1024]{0:T(1024)}, u32[]{:S(2)}) copy-start(f32[1024]{0:T(1024)} %get-tuple-element.36) | copy-start | bytes 12292
  95.6 26.8 %copy-start.10 = (bf16[128,64,16]{0,2,1:T(8,128)(2,1)S(1)}, bf16[128,64,16]{0,2,1:T(8,128)(2,1)}, u32[]{:S(2)}) copy-start(bf16[128,64,16]{0,2,1:T(8,128)(2,1)} %copy-done.9) | copy-start | bytes 786436
  124.7 27.0 %copy-start.13 = (f32[1,128,64]{1,2,0:T(8,128)S(1)}, f32[1,128,64]{1,2,0:T(8,128)}, u32[]{:S(2)}) copy-start(f32[1,128,64]{1,2,0:T(8,128)} %get-tuple-element.79) | copy-start | bytes 98308
  124.7 27.0 %copy-start.14 = (f32[1,128,64]{1,2,0:T(8,128)S(1)}, f32[1,128,64]{1,2,0:T(8,128)}, u32[]{:S(2)}) copy-start(f32[1,128,64]{1,2,0:T(8,128)} %get-tuple-element.80) | copy-start | bytes 98308
  138.2 134.9 %all-to-all-start.1 = ((bf16[128,64,16]{0,2,1:T(8,128)(2,1)}), bf16[128,64,16]{0,2,1:T(8,128)(2,1)S(1)}, u32[]{:S(2)}, u32[]{:S(2)}) async-start(bf16[128,64,16]{0,2,1:T(8,128)(2,1)} %bitcast.4), calls=%async_computation.1 | async-start | bytes 524288 | tf_op jit(solution)/shard_map/all_to_all | solution.py:188
  273.9 228.8 %all-to-all-start.10 = ((f32[64,1,1024]{2,1,0:T(1,128)}), f32[64,1,1024]{2,1,0:T(1,128)S(1)}, u32[]{:S(2)}, u32[]{:S(2)}) async-start(f32[64,1,1024]{2,1,0:T(1,128)} %broadcast_in_dim.5), calls=%async_computation.10 | async-start | bytes 524288 | tf_op jit(solution)/shard_map/all_to_all | solution.py:19
  444.7 35.3 %copy-start.15 = (f32[1,64,128]{2,1,0:T(8,128)S(1)}, f32[1,64,128]{2,1,0:T(8,128)}, u32[]{:S(2)}) copy-start(f32[1,64,128]{2,1,0:T(8,128)} %get-tuple-element.93) | copy-start | bytes 98308
  444.8 35.3 %copy-start.16 = (f32[1,64,128]{2,1,0:T(8,128)S(1)}, f32[1,64,128]{2,1,0:T(8,128)}, u32[]{:S(2)}) copy-start(f32[1,64,128]{2,1,0:T(8,128)} %get-tuple-element.94) | copy-start | bytes 98308
  502.7 20.7 %all-to-all-start.7 = ((bf16[64,128,16]{1,2,0:T(8,128)(2,1)}), bf16[64,128,16]{1,2,0:T(8,128)(2,1)S(1)}, u32[]{:S(2)}, u32[]{:S(2)}) async-start(bf16[64,128,16]{1,2,0:T(8,128)(2,1)} %copy_bitcast_fusion.3), calls=%async_computation.7 | async-start | bytes 524288 | tf_op jit(solution)/shard_map/all_to_all | solution.py:211
  521.1 68.5 %copy-start.4 = (bf16[128,1024]{0,1:T(8,128)(2,1)S(1)}, bf16[128,1024]{0,1:T(8,128)(2,1)}, u32[]{:S(2)}) copy-start(bf16[128,1024]{0,1:T(8,128)(2,1)} %copy-done.3) | copy-start | bytes 786436
  521.1 68.5 %copy-start.6 = (bf16[128,1024]{0,1:T(8,128)(2,1)S(1)}, bf16[128,1024]{0,1:T(8,128)(2,1)}, u32[]{:S(2)}) copy-start(bf16[128,1024]{0,1:T(8,128)(2,1)} %copy-done.5) | copy-start | bytes 786436
  521.1 68.5 %copy-start.8 = (bf16[128,1024]{0,1:T(8,128)(2,1)S(1)}, bf16[128,1024]{0,1:T(8,128)(2,1)}, u32[]{:S(2)}) copy-start(bf16[128,1024]{0,1:T(8,128)(2,1)} %copy-done.7) | copy-start | bytes 786436
  521.1 68.5 %copy-start.18 = (f32[1024]{0:T(1024)S(1)}, f32[1024]{0:T(1024)}, u32[]{:S(2)}) copy-start(f32[1024]{0:T(1024)} %param.17) | copy-start | bytes 12292
  523.4 19.5 %all-to-all-start.5 = ((bf16[64,128,16]{1,2,0:T(8,128)(2,1)}), bf16[64,128,16]{1,2,0:T(8,128)(2,1)S(1)}, u32[]{:S(2)}, u32[]{:S(2)}) async-start(bf16[64,128,16]{1,2,0:T(8,128)(2,1)} %bitcast.231), calls=%async_computation.5 | async-start | bytes 524288 | tf_op jit(solution)/shard_map/all_to_all | solution.py:201
  543.0 15.4 %all-to-all-start.4 = ((bf16[64,128,16]{1,2,0:T(8,128)(2,1)}), bf16[64,128,16]{1,2,0:T(8,128)(2,1)S(1)}, u32[]{:S(2)}, u32[]{:S(2)}) async-start(bf16[64,128,16]{1,2,0:T(8,128)(2,1)} %bitcast.232), calls=%async_computation.4 | async-start | bytes 524288 | tf_op jit(solution)/shard_map/all_to_all | solution.py:198
  573.4 23.3 %all-to-all-start.9 = ((bf16[4,128,256]{1,2,0:T(8,128)(2,1)}), bf16[4,128,256]{1,2,0:T(8,128)(2,1)S(1)}, u32[]{:S(2)}, u32[]{:S(2)}) async-start(bf16[4,128,256]{1,2,0:T(8,128)(2,1)} %bitcast.99), calls=%async_computation.9 | async-start | bytes 524288 | tf_op jit(solution)/shard_map/all_to_all | solution.py:37
  (5 other events, 12.6 us)
where the time goes:
time: 606 us; the launch traced here: 598 us
  matrix products  221 us (36%)
  local copies, waits for them, and re-layouts  211 us (35%)
  starting transfers between devices  91.7 us (15%)
  waiting for transfers between devices  36.7 us (6%)
  other arithmetic  21.7 us (4%)
  blocking collectives  15 us (2%)
    dot_general x3, matrix products, inner_forward(): jnp.einsum('rsjxab,sjabc->rjxbc', block_table(outer_table), values, preci...  106 us
    dot_general x2, matrix products, inner_inverse(): jnp.einsum('rsjabx,sjxbc->rjabc', block_table(outer_table), values, preci...  70.8 us
    another operation x2, local copies, waits for them, and re-layouts, block_table(): jnp.stack([jnp.stack([cosine, -sine_part]), jnp.stack([sine_part, cosine])])  52 us
    dot_general x6, local copies, waits for them, and re-layouts, leading_section(): return jnp.einsum('rkp,pmc->rkmc', table, values, precision=HIGHEST)  44.1 us
    transpose x3, local copies, waits for them, and re-layouts, inner_forward(): jnp.einsum('rsjxab,sjabc->rjxbc', block_table(outer_table), values, preci...  35.1 us
    transpose x2, local copies, waits for them, and re-layouts, inner_inverse(): jnp.einsum('rsxby,sjxyc->rjxbc', block_table(inner_table), values, precis...  30.7 us
    transpose x2, local copies, waits for them, and re-layouts, inner_inverse(): jnp.einsum('rsjabx,sjxbc->rjabc', block_table(outer_table), values, preci...  27.5 us
    all_to_all x2, starting transfers between devices, from_everyone(): return lax.all_to_all(copies, axis, split_axis=0, concat_axis=0, tiled=True)  20.6 us
  transfers between devices with their start and end apart: 10, of which 6 were waited for; matrix products, arithmetic and copies ran while one was open for 75% of the time, Pallas kernels for 0%

commit v1 on v0

v1 whole, which is shorter than its diff:
```python
import functools
import math

import jax
import jax.numpy as jnp
import numpy as np
from jax import lax
from jax.experimental import pallas as pl
from jax.experimental.pallas import tpu as pltpu
from jax.sharding import PartitionSpec as P

MESH = pl.DeviceIdType.MESH
F32 = jnp.float32
BF16 = jnp.bfloat16
ROWS = 128
SEQ = 64
HELD = 16
GROUPS = 4
PART = HELD // GROUPS
TOTAL = ROWS * SEQ
WIDTH = SEQ * HELD
QUARTER = SEQ * PART
SIGNALS = 4
DATA_LOW = True
TABLE_LOW = True


def halves(table):
    high = np.asarray(table, np.float32).astype(BF16)
    low = (np.asarray(table, np.float64) - high.astype(np.float64)).astype(np.float32).astype(BF16)
    return high, low


@functools.cache
def tables():
    row = np.arange(SEQ)
    lane = np.arange(ROWS)
    coarse = 2 * np.pi * ((row[None, :] * (4 * row[:, None] + 1)) % (4 * SEQ)) / (4 * SEQ)
    lead = np.concatenate([np.cos(coarse), -np.sin(coarse)], axis=0)
    lead = np.concatenate(halves(lead), axis=1)
    trail = np.concatenate([np.cos(coarse.T), -np.sin(coarse.T)], axis=1) / TOTAL
    trail = np.concatenate(halves(trail), axis=1)
    mid = 2 * np.pi * lane[None, :] * (4 * row[:, None] + 1) / (4 * TOTAL)
    twist = np.stack([np.cos(mid), np.sin(mid)]).astype(np.float32)
    fine = 2 * np.pi * ((lane[:, None] * lane[None, :]) % ROWS) / ROWS
    cosine, sine = np.cos(fine), np.sin(fine)
    ahead = np.stack(halves(np.block([[cosine, -sine], [sine, cosine]])))
    back = np.stack(halves(np.block([[cosine, sine], [-sine, cosine]])))
    return lead, trail, twist, ahead, back


def pack_kernel(fk, fv, bk, bv, bg, bq, fl, send, send_f, xs, fs):
    for m, (left, right) in enumerate(((fk, fv), (bk, bv), (bg, bq))):
        for b in range(WIDTH // ROWS):
            cols = slice(b * ROWS, (b + 1) * ROWS)
            xs[m, cols, :] = (left[:, cols].astype(F32) * right[:, cols].astype(F32)).T
    for b in range(QUARTER // ROWS):
        cols = slice(b * ROWS, (b + 1) * ROWS)
        fs[cols, :] = fl[:, cols].T

    def per_peer(step, carry):
        for k in range(8):
            peer = step * 8 + k
            for m in range(3):
                send[peer, m] = xs[m, pl.ds(peer, HELD, stride=SEQ), :].astype(BF16)
            send_f[peer] = fs[pl.ds(peer, PART, stride=SEQ), :].astype(BF16)
        return carry

    lax.fori_loop(0, SEQ // 8, per_peer, 0)


def pack(fk, fv, bk, bv, bg, bq, fl):
    return pl.pallas_call(
        pack_kernel,
        out_shape=(
            jax.ShapeDtypeStruct((SEQ, 3, HELD, ROWS), BF16),
            jax.ShapeDtypeStruct((SEQ, PART, ROWS), BF16),
        ),
        in_specs=[pl.BlockSpec(memory_space=pltpu.VMEM)] * 7,
        out_specs=[pl.BlockSpec(memory_space=pltpu.VMEM)] * 2,
        scratch_shapes=[pltpu.VMEM((3, WIDTH, ROWS), F32), pltpu.VMEM((QUARTER, ROWS), F32)],
    )(fk, fv, bk, bv, bg, bq, fl)


def dot(left, right):
    return jnp.dot(left, right, preferred_element_type=F32)


def split_dot(values, table):
    high = values.astype(BF16)
    total = dot(high, table[0])
    if DATA_LOW:
        total += dot((values - high.astype(F32)).astype(BF16), table[0])
    if TABLE_LOW:
        total += dot(high, table[1])
    return total


def times(a, b):
    return a[0] * b[0] - a[1] * b[1], a[0] * b[1] + a[1] * b[0]


def conj_times(a, b):
    return a[0] * b[0] + a[1] * b[1], a[0] * b[1] - a[1] * b[0]


def convolve_kernel(rx, filt, lead, trail, twist, ahead, back, y, terms, gs, xs, fs, ys, ts):
    def widen(step, carry):
        for k in range(8):
            s = step * 8 + k
            for m in range(3):
                xs[m, pl.ds(pl.multiple_of(s * HELD, HELD), HELD), :] = rx[s, m].astype(F32)
            for q in range(GROUPS):
                fs[q, pl.ds(s * PART, PART), :] = filt[q, s].astype(F32)
        return carry

    lax.fori_loop(0, SEQ // 8, widen, 0)
    gs[...] = jnp.zeros_like(gs)
    lane = lax.broadcasted_iota(jnp.int32, (1, ROWS), 1)

    def quarter(q, carry):
        chans = [(q * PART + r, r) for r in range(PART)]
        fronts = []
        for j, r in chans:
            cols = [xs[m, pl.ds(j, SEQ, stride=HELD), :] for m in range(3)]
            cols.append(fs[q, pl.ds(r, SEQ, stride=PART), :])
            total = jnp.sum(jnp.sum(cols[1] * cols[2], axis=0, keepdims=True), axis=1, keepdims=True)
            gs[...] += jnp.where(lane == j, total, 0.0)
            x = jnp.concatenate(cols, axis=1).astype(BF16)
            fronts.append(dot(lead[...], jnp.concatenate([x, x], axis=0)))
        spectra = []
        for front in fronts:
            rows = []
            for m in range(SIGNALS):
                real = front[:SEQ, m * ROWS : (m + 1) * ROWS]
                imag = front[SEQ:, m * ROWS : (m + 1) * ROWS]
                rows.append(
                    jnp.concatenate(
                        [real * twist[0] + imag * twist[1], imag * twist[0] - real * twist[1]], axis=1
                    )
                )
            spectra.append(split_dot(jnp.concatenate(rows, axis=0), ahead))
        products = []
        for spec in spectra:
            first, second, up, filt_spec = (
                (spec[m * SEQ : (m + 1) * SEQ, :ROWS], spec[m * SEQ : (m + 1) * SEQ, ROWS:])
                for m in range(SIGNALS)
            )
            made = (
                times(filt_spec, first),
                times(filt_spec, second),
                conj_times(filt_spec, up),
                conj_times(second, up),
            )
            rows = jnp.concatenate([jnp.concatenate(pair, axis=1) for pair in made], axis=0)
            products.append(split_dot(rows, back))
        for (j, r), rows in zip(chans, products):
            reals, imags = [], []
            for m in range(SIGNALS):
                real = rows[m * SEQ : (m + 1) * SEQ, :ROWS]
                imag = rows[m * SEQ : (m + 1) * SEQ, ROWS:]
                reals.append(real * twist[0] - imag * twist[1])
                imags.append(real * twist[1] + imag * twist[0])
            z = jnp.concatenate(
                [jnp.concatenate(reals, axis=1), jnp.concatenate(imags, axis=1)], axis=0
            )
            high = z.astype(BF16)
            final = dot(trail[...], jnp.concatenate([high, high], axis=0))
            if DATA_LOW:
                final += dot(trail[:, : 2 * SEQ], (z - high.astype(F32)).astype(BF16))
            for m in range(3):
                ys[m, pl.ds(j, SEQ, stride=HELD), :] = final[:, m * ROWS : (m + 1) * ROWS]
            ts[q, pl.ds(r, SEQ, stride=PART), :] = final[:, 3 * ROWS :]
        return carry

    lax.fori_loop(0, GROUPS, quarter, 0)
    gs[...] *= 1.0 / math.sqrt(TOTAL)

    def narrow(step, carry):
        for k in range(8):
            s = step * 8 + k
            for m in range(3):
                y[s, m] = ys[m, pl.ds(pl.multiple_of(s * HELD, HELD), HELD), :].astype(BF16)
        return carry

    lax.fori_loop(0, SEQ // 8, narrow, 0)
    for q in range(GROUPS):
        terms[q] = (ts[q] * (1.0 / math.sqrt(TOTAL))).astype(BF16)


def convolve(rx, filt):
    consts = [jnp.asarray(t) for t in tables()]
    return pl.pallas_call(
        convolve_kernel,
        out_shape=(
            jax.ShapeDtypeStruct((SEQ, 3, HELD, ROWS), BF16),
            jax.ShapeDtypeStruct((GROUPS, QUARTER, ROWS), BF16),
            jax.ShapeDtypeStruct((1, ROWS), F32),
        ),
        in_specs=[pl.BlockSpec(memory_space=pltpu.VMEM)] * 7,
        out_specs=[pl.BlockSpec(memory_space=pltpu.VMEM)] * 3,
        scratch_shapes=[
            pltpu.VMEM((3, WIDTH, ROWS), F32),
            pltpu.VMEM((GROUPS, QUARTER, ROWS), F32),
            pltpu.VMEM((3, WIDTH, ROWS), F32),
            pltpu.VMEM((GROUPS, QUARTER, ROWS), F32),
        ],
    )(rx, filt, *consts)


def finish_kernel(
    r, rf, rs, fq, fk, fv, bq, bk, bv, bg, skip, out, gq, gk, gv, gf, gsk, xs, fs, ss
):
    ss[...] = jnp.zeros_like(ss)

    def per_peer(step, carry):
        for k in range(8):
            peer = step * 8 + k
            for m in range(3):
                xs[m, pl.ds(peer, HELD, stride=SEQ), :] = r[peer, m].astype(F32)
            fs[pl.ds(peer, PART, stride=SEQ), :] = rf[peer].astype(F32)
            ss[pl.ds(peer, 1), :] = rs[peer]
        return carry

    lax.fori_loop(0, SEQ // 8, per_peer, 0)
    for b in range(WIDTH // ROWS):
        cols = slice(b * ROWS, (b + 1) * ROWS)
        gain = skip[:, cols]
        key, value = bk[:, cols].astype(F32), bv[:, cols].astype(F32)
        grad = bg[:, cols].astype(F32)
        source = (fk[:, cols].astype(F32) * fv[:, cols].astype(F32)).astype(BF16).astype(F32)
        second = (key * value).astype(BF16).astype(F32)
        upstream = (grad * bq[:, cols].astype(F32)).astype(BF16).astype(F32)
        out[:, cols] = (fq[:, cols].astype(F32) * (xs[0, cols, :].T + gain * source)).astype(BF16)
        gq[:, cols] = (grad * (xs[1, cols, :].T + gain * second)).astype(BF16)
        through = xs[2, cols, :].T + gain * upstream
        gk[:, cols] = (through * value).astype(BF16)
        gv[:, cols] = (through * key).astype(BF16)
    for b in range(QUARTER // ROWS):
        cols = slice(b * ROWS, (b + 1) * ROWS)
        gf[:, cols] = fs[cols, :].T
    ss[...] = ss[...].T
    even, odd = ss[pl.ds(0, 8, stride=2), :], ss[pl.ds(1, 8, stride=2), :]
    lane = lax.broadcasted_iota(jnp.int32, (8, ROWS), 1)
    gsk[...] = jnp.where(lane < SEQ, even, pltpu.roll(odd, SEQ, 1))


def finish(r, rf, rs, fq, fk, fv, bq, bk, bv, bg, skip):
    wide = jax.ShapeDtypeStruct((ROWS, WIDTH), BF16)
    return pl.pallas_call(
        finish_kernel,
        out_shape=(
            wide,
            wide,
            wide,
            wide,
            jax.ShapeDtypeStruct((ROWS, QUARTER), F32),
            jax.ShapeDtypeStruct((8, ROWS), F32),
        ),
        in_specs=[pl.BlockSpec(memory_space=pltpu.VMEM)] * 11,
        out_specs=[pl.BlockSpec(memory_space=pltpu.VMEM)] * 6,
        scratch_shapes=[
            pltpu.VMEM((3, WIDTH, ROWS), F32),
            pltpu.VMEM((QUARTER, ROWS), F32),
            pltpu.VMEM((ROWS, ROWS), F32),
        ],
    )(r, rf, rs, fq, fk, fv, bq, bk, bv, bg, skip)


def shifted(me, step):
    dz, dy, dx = step // 16, (step // 4) % 4, step % 4
    x, z, y = me // 16, (me // 4) % 4, me % 4
    return ((x + dx) % 4) * 16 + ((z + dz) % 4) * 4 + (y + dy) % 4


def greet(me, partners):
    barrier = pltpu.get_barrier_semaphore()

    def hello(step, carry):
        pl.semaphore_signal(
            barrier, inc=1, device_id={"seq": shifted(me, step)}, device_id_type=MESH
        )
        return carry

    lax.fori_loop(1, SEQ, hello, 0)
    for other in partners:
        pl.semaphore_signal(barrier, inc=1, device_id={"chan": other}, device_id_type=MESH)
    pl.semaphore_wait(barrier, SEQ - 1 + len(partners))


def push(src, dst, sems, target):
    copy = pltpu.make_async_remote_copy(
        src_ref=src,
        dst_ref=dst,
        send_sem=sems[0],
        recv_sem=sems[1],
        device_id=target,
        device_id_type=MESH,
    )
    copy.start()
    return copy


def push_all(src, dst, sems, me, first, last):
    def one(step, carry):
        peer = shifted(me, step)
        push(src.at[peer], dst.at[me], sems, {"seq": peer})
        return carry

    lax.fori_loop(first, last, one, 0)


def all_of(ref, sems, me):
    most = ref.at[pl.ds(0, SEQ - 1)]
    return pltpu.make_async_remote_copy(
        src_ref=most,
        dst_ref=most,
        send_sem=sems[0],
        recv_sem=sems[1],
        device_id={"seq": shifted(me, 1)},
        device_id_type=MESH,
    )


def partners_of(group):
    core, half = group % 2, group // 2
    return 2 * half + (1 - core), 2 * (1 - half) + core, 2 * (1 - half) + (1 - core)


def gather_kernel(send, send_f, recv, filt, s0, r0, s1, r1, s2, r2):
    me, group = lax.axis_index("seq"), lax.axis_index("chan")
    beside, across, corner = partners_of(group)
    greet(me, (beside, across))
    mine = filt.at[group]
    push_all(send_f, mine, (s1, r1), me, 1, SEQ)
    push_all(send, recv, (s0, r0), me, 1, 16)
    recv[me] = send[me]
    filt[group, me] = send_f[me]
    both = all_of(mine, (s1, r1), me)
    both.wait_recv()
    far = push(mine, mine, (s2.at[1], r2.at[1]), {"chan": across})
    near = push(mine, mine, (s2.at[0], r2.at[0]), {"chan": beside})
    push_all(send, recv, (s0, r0), me, 16, SEQ)
    far.wait_recv()
    other = filt.at[across]
    onward = push(other, other, (s2.at[2], r2.at[2]), {"chan": beside})
    near.wait_recv()
    onward.wait_recv()
    main = all_of(recv, (s0, r0), me)
    main.wait_recv()
    both.wait_send()
    far.wait_send()
    near.wait_send()
    onward.wait_send()
    main.wait_send()


def gather(send, send_f):
    return pl.pallas_call(
        gather_kernel,
        out_shape=(
            jax.ShapeDtypeStruct(send.shape, send.dtype),
            jax.ShapeDtypeStruct((GROUPS, *send_f.shape), send_f.dtype),
        ),
        in_specs=[pl.BlockSpec(memory_space=pltpu.VMEM)] * 2,
        out_specs=[pl.BlockSpec(memory_space=pltpu.VMEM)] * 2,
        scratch_shapes=[pltpu.SemaphoreType.DMA] * 4 + [pltpu.SemaphoreType.DMA((3,))] * 2,
        compiler_params=pltpu.CompilerParams(collective_id=0, has_side_effects=True),
    )(send, send_f)


def scatter_kernel(
    y, terms, gs, recv, recv_f, recv_s, near_in, far_in, far_out, total, send_f,
    s0, r0, s1, r1, s2, r2, s3, r3,
):
    me, group = lax.axis_index("seq"), lax.axis_index("chan")
    core, half = group % 2, group // 2
    beside, across, corner = partners_of(group)
    greet(me, (beside, across))
    pushed = [
        push(terms.at[2 * h + (1 - core)], near_in.at[h], (s2.at[h], r2.at[h]), {"chan": beside})
        for h in range(2)
    ]

    def skips(step, carry):
        peer = shifted(me, step)
        push(gs, recv_s.at[me], (s3, r3), {"seq": peer})
        return carry

    lax.fori_loop(1, SEQ, skips, 0)
    push_all(y, recv, (s0, r0), me, 1, 16)
    for copy in pushed:
        copy.wait_recv()
    away = 1 - half
    far_out[...] = (terms[2 * away + core].astype(F32) + near_in[away].astype(F32)).astype(BF16)
    far = push(far_out, far_in, (s2.at[2], r2.at[2]), {"chan": across})
    push_all(y, recv, (s0, r0), me, 16, SEQ)
    recv[me] = y[me]
    recv_s[me] = gs[...]
    total[...] = terms[group].astype(F32) + near_in[half].astype(F32)
    far.wait_recv()
    total[...] += far_in[...].astype(F32)

    def cut(step, carry):
        for k in range(8):
            s = step * 8 + k
            send_f[s] = total[pl.ds(s * PART, PART), :].astype(BF16)
        return carry

    lax.fori_loop(0, SEQ // 8, cut, 0)
    push_all(send_f, recv_f, (s1, r1), me, 1, SEQ)
    recv_f[me] = send_f[me]
    last = [all_of(recv, (s0, r0), me), all_of(recv_f, (s1, r1), me), all_of(recv_s, (s3, r3), me)]
    for copy in last:
        copy.wait_recv()
    for copy in last + pushed + [far]:
        copy.wait_send()


def scatter(y, terms, gs):
    return pl.pallas_call(
        scatter_kernel,
        out_shape=(
            jax.ShapeDtypeStruct(y.shape, y.dtype),
            jax.ShapeDtypeStruct((SEQ, PART, ROWS), BF16),
            jax.ShapeDtypeStruct((SEQ, 1, ROWS), F32),
        ),
        in_specs=[pl.BlockSpec(memory_space=pltpu.VMEM)] * 3,
        out_specs=[pl.BlockSpec(memory_space=pltpu.VMEM)] * 3,
        scratch_shapes=[
            pltpu.VMEM((2, QUARTER, ROWS), BF16),
            pltpu.VMEM((QUARTER, ROWS), BF16),
            pltpu.VMEM((QUARTER, ROWS), BF16),
            pltpu.VMEM((QUARTER, ROWS), F32),
            pltpu.VMEM((SEQ, PART, ROWS), BF16),
        ]
        + [pltpu.SemaphoreType.DMA] * 4
        + [pltpu.SemaphoreType.DMA((3,))] * 2
        + [pltpu.SemaphoreType.DMA] * 2,
        compiler_params=pltpu.CompilerParams(collective_id=1, has_side_effects=True),
    )(y, terms, gs)


def per_device(fwd_q, fwd_k, fwd_v, bwd_q, bwd_k, bwd_v, bwd_grad, filters, skip):
    send, send_f = pack(fwd_k, fwd_v, bwd_k, bwd_v, bwd_grad, bwd_q, filters)
    recv, filt = gather(send, send_f)
    y, terms, gs = convolve(recv, filt)
    back, back_f, back_s = scatter(y, terms, gs)
    *wide, skips = finish(
        back, back_f, back_s, fwd_q, fwd_k, fwd_v, bwd_q, bwd_k, bwd_v, bwd_grad, skip[None, :]
    )
    return (*wide, skips.reshape(WIDTH))


def solution(mesh):
    both = P("seq", "chan")
    return jax.shard_map(
        per_device,
        mesh=mesh,
        in_specs=(both,) * 8 + (P("chan"),),
        out_specs=(both,) * 5 + (P("chan"),),
        check_vma=False,
    )
```

time: 606 us -> 96.4 us (0.16); the launches traced: 598 us -> 96.2 us
  matrix products: 221 us -> 0 us
  local copies, waits for them, and re-layouts: 211 us -> 0 us
  Pallas kernels: 0 us -> 95.5 us
  starting transfers between devices: 91.7 us -> 0 us
  waiting for transfers between devices: 36.7 us -> 0 us
  other arithmetic: 21.7 us -> 0 us
  blocking collectives: 15 us -> 0 us
    dot_general x15 -> x0, matrix products: 221 us -> none  [the longest x3 106 us: inner_forward(): jnp.einsum('rsjxab,sjabc->rjxbc', block_table(outer_table), values, preci...]
    pallas_call x0 -> x5, Pallas kernels: none -> 95.5 us  [the longest x1 40.7 us: scatter(): pl.pallas_call(scatter_kernel, out_shape=(jax.ShapeDtypeStruct(y.shape, y...]
    transpose x7 -> x0, local copies, waits for them, and re-layouts: 93.3 us -> none  [the longest x3 35.1 us: inner_forward(): jnp.einsum('rsjxab,sjabc->rjxbc', block_table(outer_table), values, preci...]
    all_to_all x10 -> x0, starting transfers between devices: 91.7 us -> none  [the longest x2 20.6 us: from_everyone(): return lax.all_to_all(copies, axis, split_axis=0, concat_axis=0, tiled=True)]
    another operation x2 -> x0, local copies, waits for them, and re-layouts: 52 us -> none  [block_table(): jnp.stack([jnp.stack([cosine, -sine_part]), jnp.stack([sine_part, cosine])])]
    dot_general x6 -> x0, local copies, waits for them, and re-layouts: 44.1 us -> none  [leading_section(): return jnp.einsum('rkp,pmc->rkmc', table, values, precision=HIGHEST)]
    all_to_all x10 -> x0, waiting for transfers between devices: 36.7 us -> none  [the longest x1 10.4 us: per_device(): lax.all_to_all(shortened(conv_local[:, :narrow]), 'seq', split_axis=0, co...]
    unnamed x54 -> x0, local copies, waits for them, and re-layouts: 17 us -> none
  transfers between devices with their start and end apart: 10 -> 0, of which waited for: 6 -> 0; matrix products, arithmetic and copies ran while one was open for 75% -> 0% of each run, Pallas kernels for 0% -> 0%
where the time goes in v1:
time: 96.4 us; the launch traced here: 96.2 us
  Pallas kernels  95.5 us (99%)
    pallas_call x1, Pallas kernels, scatter(): pl.pallas_call(scatter_kernel, out_shape=(jax.ShapeDtypeStruct(y.shape, y...  40.7 us
    pallas_call x1, Pallas kernels, gather(): pl.pallas_call(gather_kernel, out_shape=(jax.ShapeDtypeStruct(send.shape,...  37.1 us
    pallas_call x1, Pallas kernels, convolve(): pl.pallas_call(convolve_kernel, out_shape=(jax.ShapeDtypeStruct((SEQ, 3,...  8.95 us
    pallas_call x1, Pallas kernels, finish(): pl.pallas_call(finish_kernel, out_shape=(wide, wide, wide, wide, jax.Shap...  4.96 us
    pallas_call x1, Pallas kernels, pack(): pl.pallas_call(pack_kernel, out_shape=(jax.ShapeDtypeStruct((SEQ, 3, HELD...  3.85 us

profile of v1, /device:TPU:1, one launch (start us, length us, event | category | flops | bytes accessed | tf_op | source)
XLA Modules:
  0.0 96.2 jit_solution(75128820659735611)
XLA Ops:
  0.6 3.8 %shard_map.181 = (bf16[64,3,16,128]{3,2,1,0:T(8,128)(2,1)}, bf16[64,4,128]{2,1,0:T(4,128)(2,1)}) custom-call(bf16[128,1024]{1,0:T(8,128)(2,1)} %fk.3, bf16[128,1024]{1,0:T(8,128)(2,1)} %fv.3, bf16[128,1024]{1,0:T(8,128)(2,1)} %bk.3, bf16[128,1024]{1,0:T(8,128)(2,1)} %bv.3, bf16[128,1024]{1,0:T(8,128)(2,1)} %bg.3, bf16[128,1024]{1,0:T(8,128)(2,1)} %bq.3, ...), custom_call_target="tpu_custom_call" | custom-call | tf_op jit(solution)/shard_map/pallas_call | solution.py:73
  4.5 37.1 %shard_map.182 = (bf16[64,3,16,128]{3,2,1,0:T(8,128)(2,1)}, bf16[4,64,4,128]{3,2,1,0:T(4,128)(2,1)}) custom-call(bf16[64,3,16,128]{3,2,1,0:T(8,128)(2,1)} %get-tuple-element.22.send, bf16[64,4,128]{2,1,0:T(4,128)(2,1)} %get-tuple-element.23.send_f), custom_call_target="tpu_custom_call" | custom-call | tf_op jit(solution)/shard_map/pallas_call | solution.py:359
  41.6 8.9 %shard_map.183 = (bf16[64,3,16,128]{3,2,1,0:T(8,128)(2,1)}, bf16[4,256,128]{2,1,0:T(8,128)(2,1)}, f32[1,128]{1,0:T(1,128)}) custom-call(bf16[64,3,16,128]{3,2,1,0:T(8,128)(2,1)} %get-tuple-element.24.rx, bf16[4,64,4,128]{3,2,1,0:T(4,128)(2,1)} %get-tuple-element.25.filt, bf16[128,128]{1,0:T(8,128)(2,1)} %constant.10.clone.lead, ...), custom_call_target="tpu_custom_call" | custom-call | tf_op jit(solution)/shard_map/pallas_call | solution.py:193
  50.5 40.7 %shard_map.184 = (bf16[64,3,16,128]{3,2,1,0:T(8,128)(2,1)}, bf16[64,4,128]{2,1,0:T(4,128)(2,1)}, f32[64,1,128]{2,1,0:T(1,128)}) custom-call(bf16[64,3,16,128]{3,2,1,0:T(8,128)(2,1)} %get-tuple-element.26.y, bf16[4,256,128]{2,1,0:T(8,128)(2,1)} %get-tuple-element.27.terms, f32[1,128]{1,0:T(1,128)} %get-tuple-element.28.gs), custom_call_target="tpu_custom_call" | custom-call | tf_op jit(solution)/shard_map/pallas_call | solution.py:421
  91.2 5.0 %shard_map.185 = (bf16[128,1024]{1,0:T(8,128)(2,1)}, bf16[128,1024]{1,0:T(8,128)(2,1)}, bf16[128,1024]{1,0:T(8,128)(2,1)}, bf16[128,1024]{1,0:T(8,128)(2,1)}, f32[128,256]{1,0:T(8,128)}, /*index=5*/f32[8,128]{1,0:T(8,128)}) custom-call(bf16[64,3,16,128]{3,2,1,0:T(8,128)(2,1)} %get-tuple-element.29.r, bf16[64,4,128]{2,1,0:T(4,128)(2,1)} %get-tuple-element.30.rf, ...), custom_call_target="tpu_custom_call" | custom-call | tf_op jit(solution)/shard_map/pallas_call | solution.py:250

commit v2 on v1

v2 whole, which is shorter than its diff:
```python
import functools
import math

import jax
import jax.numpy as jnp
import numpy as np
from jax import lax
from jax.experimental import pallas as pl
from jax.experimental.pallas import tpu as pltpu
from jax.sharding import PartitionSpec as P

MESH = pl.DeviceIdType.MESH
F32 = jnp.float32
BF16 = jnp.bfloat16
ROWS = 128
SEQ = 64
HELD = 16
GROUPS = 4
PART = HELD // GROUPS
TOTAL = ROWS * SEQ
WIDTH = SEQ * HELD
QUARTER = SEQ * PART
SIGNALS = 4
DATA_LOW = True
TABLE_LOW = True


def halves(table):
    high = np.asarray(table, np.float32).astype(BF16)
    low = (np.asarray(table, np.float64) - high.astype(np.float64)).astype(np.float32).astype(BF16)
    return high, low


@functools.cache
def tables():
    row = np.arange(SEQ)
    lane = np.arange(ROWS)
    coarse = 2 * np.pi * ((row[None, :] * (4 * row[:, None] + 1)) % (4 * SEQ)) / (4 * SEQ)
    lead = np.concatenate([np.cos(coarse), -np.sin(coarse)], axis=0)
    lead = np.concatenate(halves(lead), axis=1)
    trail = np.concatenate([np.cos(coarse.T), -np.sin(coarse.T)], axis=1) / TOTAL
    trail = np.concatenate(halves(trail), axis=1)
    mid = 2 * np.pi * lane[None, :] * (4 * row[:, None] + 1) / (4 * TOTAL)
    twist = np.stack([np.cos(mid), np.sin(mid)]).astype(np.float32)
    fine = 2 * np.pi * ((lane[:, None] * lane[None, :]) % ROWS) / ROWS
    cosine, sine = np.cos(fine), np.sin(fine)
    ahead = np.stack(halves(np.block([[cosine, -sine], [sine, cosine]])))
    back = np.stack(halves(np.block([[cosine, sine], [-sine, cosine]])))
    return lead, trail, twist, ahead, back


def dot(left, right):
    return jnp.dot(left, right, preferred_element_type=F32)


def split_dot(values, table):
    high = values.astype(BF16)
    total = dot(high, table[0])
    if DATA_LOW:
        total += dot((values - high.astype(F32)).astype(BF16), table[0])
    if TABLE_LOW:
        total += dot(high, table[1])
    return total


def times(a, b):
    return a[0] * b[0] - a[1] * b[1], a[0] * b[1] + a[1] * b[0]


def conj_times(a, b):
    return a[0] * b[0] + a[1] * b[1], a[0] * b[1] - a[1] * b[0]


def forward(cols, lead, twist, ahead):
    x = jnp.concatenate(cols, axis=1).astype(BF16)
    front = dot(lead[...], jnp.concatenate([x, x], axis=0))
    rows = []
    for m in range(len(cols)):
        real, imag = front[:SEQ, m * ROWS : (m + 1) * ROWS], front[SEQ:, m * ROWS : (m + 1) * ROWS]
        turned = [real * twist[0] + imag * twist[1], imag * twist[0] - real * twist[1]]
        rows.append(jnp.concatenate(turned, axis=1))
    spec = split_dot(jnp.concatenate(rows, axis=0), ahead)
    return [spec[m * SEQ : (m + 1) * SEQ] for m in range(len(cols))]


def inverse(pairs, trail, twist, back):
    rows = jnp.concatenate([jnp.concatenate(pair, axis=1) for pair in pairs], axis=0)
    rows = split_dot(rows, back)
    reals, imags = [], []
    for m in range(len(pairs)):
        real, imag = rows[m * SEQ : (m + 1) * SEQ, :ROWS], rows[m * SEQ : (m + 1) * SEQ, ROWS:]
        reals.append(real * twist[0] - imag * twist[1])
        imags.append(real * twist[1] + imag * twist[0])
    z = jnp.concatenate([jnp.concatenate(reals, axis=1), jnp.concatenate(imags, axis=1)], axis=0)
    high = z.astype(BF16)
    final = dot(trail[...], jnp.concatenate([high, high], axis=0))
    if DATA_LOW:
        final += dot(trail[:, : 2 * SEQ], (z - high.astype(F32)).astype(BF16))
    return [final[:, m * ROWS : (m + 1) * ROWS] for m in range(len(pairs))]


def pair_of(spec):
    return spec[:, :ROWS], spec[:, ROWS:]


def rows_of(s, count):
    return pl.ds(pl.multiple_of(s * count, count), count)


def in_steps(body):
    def step(n, carry):
        for k in range(8):
            body(n * 8 + k)
        return carry

    lax.fori_loop(0, SEQ // 8, step, 0)


def every_peer(me, body, itself=False):
    x, z, y = me // 16, (me // 4) % 4, me % 4
    zs = [((z + d) % 4) * 4 for d in range(4)]
    ys = [(y + d) % 4 for d in range(4)]
    steps = [(dz, dy) for dz in (2, 1, 3, 0) for dy in range(4)]

    def plane(dx, carry):
        base = ((x + dx) % 4) * 16
        for dz, dy in steps:
            body(base + zs[dz] + ys[dy])
        return carry

    for dz, dy in steps:
        if itself or (dz, dy) != (0, 0):
            body(x * 16 + zs[dz] + ys[dy])
    lax.fori_loop(1, 4, plane, 0)


def push(src, dst, sems, target):
    copy = pltpu.make_async_remote_copy(
        src_ref=src,
        dst_ref=dst,
        send_sem=sems[0],
        recv_sem=sems[1],
        device_id=target,
        device_id_type=MESH,
    )
    copy.start()
    return copy


def main_kernel(
    fk, fv, bk, bv, bg, bq, fl, lead, trail, twist, ahead, back,
    r, rf, rs,
    send, send_f, recv, filt, xs, fs, spectra, y, terms, near_in, out_f, gs, sent, got,
):
    me, group = lax.axis_index("seq"), lax.axis_index("chan")
    core, half = group % 2, group // 2
    beside, across = 2 * half + (1 - core), 2 * (1 - half) + core
    barrier = pltpu.get_barrier_semaphore()

    def hello(seq, chan):
        pl.semaphore_signal(
            barrier, inc=1, device_id={"seq": seq, "chan": chan}, device_id_type=MESH
        )

    every_peer(me, lambda peer: hello(peer, group))
    every_peer(me, lambda peer: hello(peer, across), True)
    hello(me, beside)

    def sems(n):
        return sent.at[n], got.at[n]

    def waiting(ref, n):
        return pltpu.make_async_remote_copy(
            src_ref=ref,
            dst_ref=ref,
            send_sem=sent.at[n],
            recv_sem=got.at[n],
            device_id={"chan": beside},
            device_id_type=MESH,
        )

    def most(ref):
        return ref.at[pl.ds(0, SEQ - 1)]

    def pack(m, left, right):
        for b in range(WIDTH // ROWS):
            cols = slice(b * ROWS, (b + 1) * ROWS)
            xs[m, cols, :] = (left[:, cols].astype(F32) * right[:, cols].astype(F32)).T

        def one(peer):
            send[m, peer] = xs[m, pl.ds(peer, HELD, stride=SEQ), :].astype(BF16)

        in_steps(one)

    def send_signal(m):
        every_peer(
            me, lambda peer: push(send.at[m, peer], recv.at[m, me], sems(m), {"seq": peer})
        )
        recv[m, me] = send[m, me]

    def widen(m):
        waiting(most(recv.at[m]), m).wait_recv()

        def one(s):
            xs[m, rows_of(s, HELD), :] = recv[m, s].astype(F32)

        in_steps(one)

    def send_back(m):
        def one(s):
            y[m, s] = xs[m, rows_of(s, HELD), :].astype(BF16)

        in_steps(one)
        every_peer(
            me, lambda peer: push(y.at[m, peer], r.at[m, me], sems(3 + m), {"seq": peer})
        )
        r[m, me] = y[m, me]

    for b in range(QUARTER // ROWS):
        cols = slice(b * ROWS, (b + 1) * ROWS)
        fs[0, cols, :] = fl[:, cols].T

    def filter_rows(peer):
        send_f[peer] = fs[0, pl.ds(peer, PART, stride=SEQ), :].astype(BF16)

    in_steps(filter_rows)
    pack(1, bk, bv)
    pl.semaphore_wait(barrier, 2 * SEQ)
    landing = filt.at[group, me]
    every_peer(me, lambda peer: push(send_f.at[peer], landing, sems(6), {"seq": peer}))
    every_peer(
        me,
        lambda peer: push(send_f.at[peer], landing, sems(7), {"seq": peer, "chan": across}),
        True,
    )
    filt[group, me] = send_f[me]
    send_signal(1)
    pack(2, bg, bq)
    send_signal(2)
    pack(0, fk, fv)
    send_signal(0)
    waiting(most(filt.at[group]), 6).wait_recv()
    waiting(filt.at[across], 7).wait_recv()
    moved = [
        push(filt.at[group], filt.at[group], sems(8), {"chan": beside}),
        push(filt.at[across], filt.at[across], sems(9), {"chan": beside}),
    ]
    for copy in moved:
        copy.wait_recv()

    def filter_wide(s):
        for q in range(GROUPS):
            fs[q, pl.ds(s * PART, PART), :] = filt[q, s].astype(F32)

    in_steps(filter_wide)

    def column(m, j):
        return xs[m, pl.ds(j, SEQ, stride=HELD), :]

    def store(m, j, value):
        xs[m, pl.ds(j, SEQ, stride=HELD), :] = value

    widen(1)

    def second(q, carry):
        cols = [column(1, q * PART + k) for k in range(PART)]
        cols += [fs[q, pl.ds(k, SEQ, stride=PART), :] for k in range(PART)]
        spec = forward(cols, lead, twist, ahead)
        pairs = []
        for k in range(PART):
            spectra[0, q * PART + k] = spec[k]
            spectra[1, q * PART + k] = spec[PART + k]
            pairs.append(times(pair_of(spec[PART + k]), pair_of(spec[k])))
        for k, value in enumerate(inverse(pairs, trail, twist, back)):
            store(3, q * PART + k, value)
        return carry

    lax.fori_loop(0, GROUPS, second, 0)

    def second_out(s):
        y[1, s] = xs[3, rows_of(s, HELD), :].astype(BF16)

    in_steps(second_out)
    every_peer(me, lambda peer: push(y.at[1, peer], r.at[1, me], sems(4), {"seq": peer}))
    r[1, me] = y[1, me]

    widen(2)
    gs[...] = jnp.zeros_like(gs)
    lane = lax.broadcasted_iota(jnp.int32, (1, ROWS), 1)
    scale = 1.0 / math.sqrt(TOTAL)

    def correlate(q, carry):
        cols = [column(2, q * PART + k) for k in range(PART)]
        for k in range(PART):
            part = jnp.sum(cols[k] * column(1, q * PART + k), axis=0, keepdims=True)
            part = jnp.sum(part, axis=1, keepdims=True)
            gs[...] += jnp.where(lane == q * PART + k, part * scale, 0.0)
        spec = forward(cols, lead, twist, ahead)
        pairs = []
        for k in range(PART):
            pairs.append(conj_times(pair_of(spectra[1, q * PART + k]), pair_of(spec[k])))
        for k in range(PART):
            pairs.append(conj_times(pair_of(spectra[0, q * PART + k]), pair_of(spec[k])))
        values = inverse(pairs, trail, twist, back)
        for k in range(PART):
            store(2, q * PART + k, values[k])
            fs[q, pl.ds(k, SEQ, stride=PART), :] = values[PART + k]
        return carry

    lax.fori_loop(0, GROUPS, correlate, 0)
    for q in range(GROUPS):
        terms[q] = (fs[q] * scale).astype(BF16)
    swapped = [
        push(terms.at[2 * h + (1 - core)], near_in.at[h], sems(10 + h), {"chan": beside})
        for h in range(2)
    ]
    send_back(2)
    for copy in swapped:
        copy.wait_recv()
    fs[0] = terms[group].astype(F32) + near_in[half].astype(F32)
    fs[1] = terms[across].astype(F32) + near_in[1 - half].astype(F32)

    def cut(s):
        for n in range(2):
            out_f[n, s] = fs[n, pl.ds(s * PART, PART), :].astype(BF16)

    in_steps(cut)

    def own_terms(peer):
        push(out_f.at[0, peer], rf.at[0, me], sems(12), {"seq": peer})
        push(gs, rs.at[me], sems(14), {"seq": peer})

    every_peer(me, own_terms)
    every_peer(
        me,
        lambda peer: push(
            out_f.at[1, peer], rf.at[1, me], sems(13), {"seq": peer, "chan": across}
        ),
        True,
    )
    rf[0, me] = out_f[0, me]
    rs[me] = gs[...]

    widen(0)

    def first(q, carry):
        cols = [column(0, q * PART + k) for k in range(PART)]
        spec = forward(cols, lead, twist, ahead)
        pairs = [
            times(pair_of(spectra[1, q * PART + k]), pair_of(spec[k])) for k in range(PART)
        ]
        for k, value in enumerate(inverse(pairs, trail, twist, back)):
            store(0, q * PART + k, value)
        return carry

    lax.fori_loop(0, GROUPS, first, 0)
    send_back(0)

    last = [waiting(most(r.at[m]), 3 + m) for m in range(3)]
    last += [waiting(most(rf.at[0]), 12), waiting(rf.at[1], 13), waiting(most(rs), 14)]
    for copy in last:
        copy.wait_recv()
    for m in range(3):
        waiting(most(send.at[m]), m).wait_send()
    waiting(most(send_f), 6).wait_send()
    waiting(send_f, 7).wait_send()
    for copy in moved + swapped + last:
        copy.wait_send()


def exchange(fk, fv, bk, bv, bg, bq, fl):
    consts = [jnp.asarray(t) for t in tables()]
    return pl.pallas_call(
        main_kernel,
        out_shape=(
            jax.ShapeDtypeStruct((3, SEQ, HELD, ROWS), BF16),
            jax.ShapeDtypeStruct((2, SEQ, PART, ROWS), BF16),
            jax.ShapeDtypeStruct((SEQ, 1, ROWS), F32),
        ),
        in_specs=[pl.BlockSpec(memory_space=pltpu.VMEM)] * 12,
        out_specs=[pl.BlockSpec(memory_space=pltpu.VMEM)] * 3,
        scratch_shapes=[
            pltpu.VMEM((3, SEQ, HELD, ROWS), BF16),
            pltpu.VMEM((SEQ, PART, ROWS), BF16),
            pltpu.VMEM((3, SEQ, HELD, ROWS), BF16),
            pltpu.VMEM((GROUPS, SEQ, PART, ROWS), BF16),
            pltpu.VMEM((4, WIDTH, ROWS), F32),
            pltpu.VMEM((GROUPS, QUARTER, ROWS), F32),
            pltpu.VMEM((2, HELD, SEQ, 2 * ROWS), F32),
            pltpu.VMEM((3, SEQ, HELD, ROWS), BF16),
            pltpu.VMEM((GROUPS, QUARTER, ROWS), BF16),
            pltpu.VMEM((2, QUARTER, ROWS), BF16),
            pltpu.VMEM((2, SEQ, PART, ROWS), BF16),
            pltpu.VMEM((1, ROWS), F32),
            pltpu.SemaphoreType.DMA((15,)),
            pltpu.SemaphoreType.DMA((15,)),
        ],
        compiler_params=pltpu.CompilerParams(collective_id=0, has_side_effects=True),
    )(fk, fv, bk, bv, bg, bq, fl, *consts)


def finish_kernel(
    r, rf, rs, fq, fk, fv, bq, bk, bv, bg, skip, out, gq, gk, gv, gf, gsk, xs, fs, ss
):
    ss[...] = jnp.zeros_like(ss)

    def per_peer(step, carry):
        for k in range(8):
            peer = step * 8 + k
            for m in range(3):
                xs[m, pl.ds(peer, HELD, stride=SEQ), :] = r[m, peer].astype(F32)
            fs[pl.ds(peer, PART, stride=SEQ), :] = rf[0, peer].astype(F32) + rf[1, peer].astype(F32)
            ss[pl.ds(peer, 1), :] = rs[peer]
        return carry

    lax.fori_loop(0, SEQ // 8, per_peer, 0)
    for b in range(WIDTH // ROWS):
        cols = slice(b * ROWS, (b + 1) * ROWS)
        gain = skip[:, cols]
        key, value = bk[:, cols].astype(F32), bv[:, cols].astype(F32)
        grad = bg[:, cols].astype(F32)
        source = (fk[:, cols].astype(F32) * fv[:, cols].astype(F32)).astype(BF16).astype(F32)
        second = (key * value).astype(BF16).astype(F32)
        upstream = (grad * bq[:, cols].astype(F32)).astype(BF16).astype(F32)
        out[:, cols] = (fq[:, cols].astype(F32) * (xs[0, cols, :].T + gain * source)).astype(BF16)
        gq[:, cols] = (grad * (xs[1, cols, :].T + gain * second)).astype(BF16)
        through = xs[2, cols, :].T + gain * upstream
        gk[:, cols] = (through * value).astype(BF16)
        gv[:, cols] = (through * key).astype(BF16)
    for b in range(QUARTER // ROWS):
        cols = slice(b * ROWS, (b + 1) * ROWS)
        gf[:, cols] = fs[cols, :].T
    ss[...] = ss[...].T
    even, odd = ss[pl.ds(0, 8, stride=2), :], ss[pl.ds(1, 8, stride=2), :]
    lane = lax.broadcasted_iota(jnp.int32, (8, ROWS), 1)
    gsk[...] = jnp.where(lane < SEQ, even, pltpu.roll(odd, SEQ, 1))


def finish(r, rf, rs, fq, fk, fv, bq, bk, bv, bg, skip):
    wide = jax.ShapeDtypeStruct((ROWS, WIDTH), BF16)
    return pl.pallas_call(
        finish_kernel,
        out_shape=(
            wide,
            wide,
            wide,
            wide,
            jax.ShapeDtypeStruct((ROWS, QUARTER), F32),
            jax.ShapeDtypeStruct((8, ROWS), F32),
        ),
        in_specs=[pl.BlockSpec(memory_space=pltpu.VMEM)] * 11,
        out_specs=[pl.BlockSpec(memory_space=pltpu.VMEM)] * 6,
        scratch_shapes=[
            pltpu.VMEM((3, WIDTH, ROWS), F32),
            pltpu.VMEM((QUARTER, ROWS), F32),
            pltpu.VMEM((ROWS, ROWS), F32),
        ],
    )(r, rf, rs, fq, fk, fv, bq, bk, bv, bg, skip)


def per_device(fwd_q, fwd_k, fwd_v, bwd_q, bwd_k, bwd_v, bwd_grad, filters, skip):
    back, back_f, back_s = exchange(fwd_k, fwd_v, bwd_k, bwd_v, bwd_grad, bwd_q, filters)
    *wide, skips = finish(
        back, back_f, back_s, fwd_q, fwd_k, fwd_v, bwd_q, bwd_k, bwd_v, bwd_grad, skip[None, :]
    )
    return (*wide, skips.reshape(WIDTH))


def solution(mesh):
    both = P("seq", "chan")
    return jax.shard_map(
        per_device,
        mesh=mesh,
        in_specs=(both,) * 8 + (P("chan"),),
        out_specs=(both,) * 5 + (P("chan"),),
        check_vma=False,
    )
```

time: 96.4 us -> 65.8 us (0.68)
  Pallas kernels: 95.5 us -> 65 us
    pallas_call x4 -> x1, Pallas kernels: 90.5 us -> 60.1 us  [exchange(): pl.pallas_call(main_kernel, out_shape=(jax.ShapeDtypeStruct((3, SEQ, HELD...]
where the time goes in v2:
time: 65.8 us; the launch traced here: 65.6 us
  Pallas kernels  65 us (99%)
    pallas_call x1, Pallas kernels, exchange(): pl.pallas_call(main_kernel, out_shape=(jax.ShapeDtypeStruct((3, SEQ, HELD...  60.1 us
    pallas_call x1, Pallas kernels, finish(): pl.pallas_call(finish_kernel, out_shape=(wide, wide, wide, wide, jax.Shap...  4.94 us

profile of v2, /device:TPU:1, one launch (start us, length us, event | category | flops | bytes accessed | tf_op | source)
XLA Modules:
  0.0 65.6 jit_solution(7273668583121527036)
XLA Ops:
  0.6 60.1 %shard_map.181 = (bf16[3,64,16,128]{3,2,1,0:T(8,128)(2,1)}, bf16[2,64,4,128]{3,2,1,0:T(4,128)(2,1)}, f32[64,1,128]{2,1,0:T(1,128)}) custom-call(bf16[128,1024]{1,0:T(8,128)(2,1)} %fk.3, bf16[128,1024]{1,0:T(8,128)(2,1)} %fv.3, bf16[128,1024]{1,0:T(8,128)(2,1)} %bk.3, bf16[128,1024]{1,0:T(8,128)(2,1)} %bv.3, bf16[128,1024]{1,0:T(8,128)(2,1)} %bg.3, ...), custom_call_target="tpu_custom_call" | custom-call | tf_op jit(solution)/shard_map/pallas_call | solution.py:373
  60.7 4.9 %shard_map.182 = (bf16[128,1024]{1,0:T(8,128)(2,1)}, bf16[128,1024]{1,0:T(8,128)(2,1)}, bf16[128,1024]{1,0:T(8,128)(2,1)}, bf16[128,1024]{1,0:T(8,128)(2,1)}, f32[128,256]{1,0:T(8,128)}, /*index=5*/f32[8,128]{1,0:T(8,128)}) custom-call(bf16[3,64,16,128]{3,2,1,0:T(8,128)(2,1)} %get-tuple-element.15.r, bf16[2,64,4,128]{3,2,1,0:T(4,128)(2,1)} %get-tuple-element.16.rf, ...), custom_call_target="tpu_custom_call" | custom-call | tf_op jit(solution)/shard_map/pallas_call | solution.py:441

commit v3 on v2

--- a/solution.py
+++ b/solution.py
@@ -20,7 +20,7 @@
 TOTAL = ROWS * SEQ
 WIDTH = SEQ * HELD
 QUARTER = SEQ * PART
-SIGNALS = 4
+COPIED = 14
 DATA_LOW = True
 TABLE_LOW = True
 
@@ -118,20 +118,24 @@
 
 def every_peer(me, body, itself=False):
     x, z, y = me // 16, (me // 4) % 4, me % 4
-    zs = [((z + d) % 4) * 4 for d in range(4)]
-    ys = [(y + d) % 4 for d in range(4)]
-    steps = [(dz, dy) for dz in (2, 1, 3, 0) for dy in range(4)]
-
-    def plane(dx, carry):
-        base = ((x + dx) % 4) * 16
-        for dz, dy in steps:
-            body(base + zs[dz] + ys[dy])
+    ys = [(y + d) % 4 for d in (2, 1, 3, 0)]
+    for other in (3 - z, (z + 2) % 4, z + 1 - 2 * (z % 2)):
+
+        def plane(dx, carry, other=other):
+            for y_other in ys:
+                body(((x + dx) % 4) * 16 + other * 4 + y_other)
+            return carry
+
+        lax.fori_loop(0, 4, plane, 0)
+
+    def level(dx, carry):
+        for y_other in ys:
+            body(((x + dx) % 4) * 16 + z * 4 + y_other)
         return carry
 
-    for dz, dy in steps:
-        if itself or (dz, dy) != (0, 0):
-            body(x * 16 + zs[dz] + ys[dy])
-    lax.fori_loop(1, 4, plane, 0)
+    lax.fori_loop(1, 4, level, 0)
+    for y_other in ys if itself else ys[:3]:
+        body(x * 16 + z * 4 + y_other)
 
 
 def push(src, dst, sems, target):
@@ -147,23 +151,31 @@
     return copy
 
 
-def main_kernel(
-    fk, fv, bk, bv, bg, bq, fl, lead, trail, twist, ahead, back,
-    r, rf, rs,
-    send, send_f, recv, filt, xs, fs, spectra, y, terms, near_in, out_f, gs, sent, got,
-):
+def main_kernel(*refs):
+    sources, (out, gq, gk, gv, gf, gsk) = refs[:COPIED], refs[COPIED : COPIED + 6]
+    copied, loaded = refs[COPIED + 6 : 2 * COPIED + 6], refs[2 * COPIED + 6]
+    (
+        r, rf, rs, send, send_f, recv, filt, xs, fs, ss, spectra, y, terms, near_in, out_f, gs,
+        sent, got,
+    ) = refs[2 * COPIED + 7 :]
+    fl, bk, bv, bg, bq, fk, fv, lead, trail, twist, ahead, back, fq, skip = copied
     me, group = lax.axis_index("seq"), lax.axis_index("chan")
     core, half = group % 2, group // 2
     beside, across = 2 * half + (1 - core), 2 * (1 - half) + core
     barrier = pltpu.get_barrier_semaphore()
+    loads = [
+        pltpu.make_async_copy(sources[n], copied[n], loaded.at[n]) for n in range(COPIED)
+    ]
+    for load in loads:
+        load.start()
 
     def hello(seq, chan):
         pl.semaphore_signal(
             barrier, inc=1, device_id={"seq": seq, "chan": chan}, device_id_type=MESH
         )
 
+    every_peer(me, lambda peer: hello(peer, across), True)
     every_peer(me, lambda peer: hello(peer, group))
-    every_peer(me, lambda peer: hello(peer, across), True)
     hello(me, beside)
 
     def sems(n):
@@ -216,6 +228,7 @@
         )
         r[m, me] = y[m, me]
 
+    loads[0].wait()
     for b in range(QUARTER // ROWS):
         cols = slice(b * ROWS, (b + 1) * ROWS)
         fs[0, cols, :] = fl[:, cols].T
@@ -224,6 +237,8 @@
         send_f[peer] = fs[0, pl.ds(peer, PART, stride=SEQ), :].astype(BF16)
 
     in_steps(filter_rows)
+    loads[1].wait()
+    loads[2].wait()
     pack(1, bk, bv)
     pl.semaphore_wait(barrier, 2 * SEQ)
     landing = filt.at[group, me]
@@ -235,10 +250,16 @@
     )
     filt[group, me] = send_f[me]
     send_signal(1)
+    loads[3].wait()
+    loads[4].wait()
     pack(2, bg, bq)
     send_signal(2)
+    loads[5].wait()
+    loads[6].wait()
     pack(0, fk, fv)
     send_signal(0)
+    for load in loads[7:]:
+        load.wait()
     waiting(most(filt.at[group]), 6).wait_recv()
     waiting(filt.at[across], 7).wait_recv()
     moved = [
@@ -257,7 +278,7 @@
     def column(m, j):
         return xs[m, pl.ds(j, SEQ, stride=HELD), :]
 
-    def store(m, j, value):
+    def put(m, j, value):
         xs[m, pl.ds(j, SEQ, stride=HELD), :] = value
 
     widen(1)
@@ -272,7 +293,7 @@
             spectra[1, q * PART + k] = spec[PART + k]
             pairs.append(times(pair_of(spec[PART + k]), pair_of(spec[k])))
         for k, value in enumerate(inverse(pairs, trail, twist, back)):
-            store(3, q * PART + k, value)
+            put(3, q * PART + k, value)
         return carry
 
     lax.fori_loop(0, GROUPS, second, 0)
@@ -303,7 +324,7 @@
             pairs.append(conj_times(pair_of(spectra[0, q * PART + k]), pair_of(spec[k])))
         values = inverse(pairs, trail, twist, back)
         for k in range(PART):
-            store(2, q * PART + k, values[k])
+            put(2, q * PART + k, values[k])
             fs[q, pl.ds(k, SEQ, stride=PART), :] = values[PART + k]
         return carry
 
@@ -350,42 +371,90 @@
             times(pair_of(spectra[1, q * PART + k]), pair_of(spec[k])) for k in range(PART)
         ]
         for k, value in enumerate(inverse(pairs, trail, twist, back)):
-            store(0, q * PART + k, value)
+            put(0, q * PART + k, value)
         return carry
 
     lax.fori_loop(0, GROUPS, first, 0)
     send_back(0)
 
-    last = [waiting(most(r.at[m]), 3 + m) for m in range(3)]
-    last += [waiting(most(rf.at[0]), 12), waiting(rf.at[1], 13), waiting(most(rs), 14)]
+    def unpack(m):
+        waiting(most(r.at[m]), 3 + m).wait_recv()
+
+        def one(peer):
+            xs[m, pl.ds(peer, HELD, stride=SEQ), :] = r[m, peer].astype(F32)
+
+        in_steps(one)
+
+    def product(left, right):
+        return (left.astype(F32) * right.astype(F32)).astype(BF16).astype(F32)
+
+    blocks = [slice(b * ROWS, (b + 1) * ROWS) for b in range(WIDTH // ROWS)]
+    unpack(1)
+    for cols in blocks:
+        mixed = xs[1, cols, :].T + skip[:, cols] * product(bk[:, cols], bv[:, cols])
+        gq[:, cols] = (bg[:, cols].astype(F32) * mixed).astype(BF16)
+    unpack(2)
+    for cols in blocks:
+        through = xs[2, cols, :].T + skip[:, cols] * product(bg[:, cols], bq[:, cols])
+        gk[:, cols] = (through * bv[:, cols].astype(F32)).astype(BF16)
+        gv[:, cols] = (through * bk[:, cols].astype(F32)).astype(BF16)
+    last = [waiting(most(rf.at[0]), 12), waiting(rf.at[1], 13), waiting(most(rs), 14)]
     for copy in last:
         copy.wait_recv()
+    ss[...] = jnp.zeros_like(ss)
+
+    def unpack_terms(peer):
+        fs[0, pl.ds(peer, PART, stride=SEQ), :] = rf[0, peer].astype(F32) + rf[1, peer].astype(F32)
+        ss[pl.ds(peer, 1), :] = rs[peer]
+
+    in_steps(unpack_terms)
+    for cols in blocks[: QUARTER // ROWS]:
+        gf[:, cols] = fs[0, cols, :].T
+    ss[...] = ss[...].T
+    even, odd = ss[pl.ds(0, 8, stride=2), :], ss[pl.ds(1, 8, stride=2), :]
+    wide = lax.broadcasted_iota(jnp.int32, (8, ROWS), 1)
+    gsk[...] = jnp.where(wide < SEQ, even, pltpu.roll(odd, SEQ, 1))
+    unpack(0)
+    for cols in blocks:
+        mixed = xs[0, cols, :].T + skip[:, cols] * product(fk[:, cols], fv[:, cols])
+        out[:, cols] = (fq[:, cols].astype(F32) * mixed).astype(BF16)
     for m in range(3):
         waiting(most(send.at[m]), m).wait_send()
+        waiting(most(r.at[m]), 3 + m).wait_send()
     waiting(most(send_f), 6).wait_send()
     waiting(send_f, 7).wait_send()
     for copy in moved + swapped + last:
         copy.wait_send()
 
 
-def exchange(fk, fv, bk, bv, bg, bq, fl):
-    consts = [jnp.asarray(t) for t in tables()]
+def exchange(fl, bk, bv, bg, bq, fk, fv, fq, skip):
+    values = (fl, bk, bv, bg, bq, fk, fv, *[jnp.asarray(t) for t in tables()], fq, skip)
+    wide = pltpu.VMEM((ROWS, WIDTH), BF16)
     return pl.pallas_call(
         main_kernel,
         out_shape=(
-            jax.ShapeDtypeStruct((3, SEQ, HELD, ROWS), BF16),
-            jax.ShapeDtypeStruct((2, SEQ, PART, ROWS), BF16),
-            jax.ShapeDtypeStruct((SEQ, 1, ROWS), F32),
+            wide,
+            wide,
+            wide,
+            wide,
+            pltpu.VMEM((ROWS, QUARTER), F32),
+            pltpu.VMEM((8, ROWS), F32),
         ),
-        in_specs=[pl.BlockSpec(memory_space=pltpu.VMEM)] * 12,
-        out_specs=[pl.BlockSpec(memory_space=pltpu.VMEM)] * 3,
+        in_specs=[pl.BlockSpec(memory_space=pltpu.HBM)] * COPIED,
+        out_specs=[pl.BlockSpec(memory_space=pltpu.VMEM)] * 6,
         scratch_shapes=[
+            *[pltpu.VMEM(v.shape, v.dtype) for v in values],
+            pltpu.SemaphoreType.DMA((COPIED,)),
+            pltpu.VMEM((3, SEQ, HELD, ROWS), BF16),
+            pltpu.VMEM((2, SEQ, PART, ROWS), BF16),
+            pltpu.VMEM((SEQ, 1, ROWS), F32),
             pltpu.VMEM((3, SEQ, HELD, ROWS), BF16),
             pltpu.VMEM((SEQ, PART, ROWS), BF16),
             pltpu.VMEM((3, SEQ, HELD, ROWS), BF16),
             pltpu.VMEM((GROUPS, SEQ, PART, ROWS), BF16),
             pltpu.VMEM((4, WIDTH, ROWS), F32),
             pltpu.VMEM((GROUPS, QUARTER, ROWS), F32),
+            pltpu.VMEM((ROWS, ROWS), F32),
             pltpu.VMEM((2, HELD, SEQ, 2 * ROWS), F32),
             pltpu.VMEM((3, SEQ, HELD, ROWS), BF16),
             pltpu.VMEM((GROUPS, QUARTER, ROWS), BF16),
@@ -396,73 +465,36 @@
             pltpu.SemaphoreType.DMA((15,)),
         ],
         compiler_params=pltpu.CompilerParams(collective_id=0, has_side_effects=True),
-    )(fk, fv, bk, bv, bg, bq, fl, *consts)
-
-
-def finish_kernel(
-    r, rf, rs, fq, fk, fv, bq, bk, bv, bg, skip, out, gq, gk, gv, gf, gsk, xs, fs, ss
-):
-    ss[...] = jnp.zeros_like(ss)
-
-    def per_peer(step, carry):
-        for k in range(8):
-            peer = step * 8 + k
-            for m in range(3):
-                xs[m, pl.ds(peer, HELD, stride=SEQ), :] = r[m, peer].astype(F32)
-            fs[pl.ds(peer, PART, stride=SEQ), :] = rf[0, peer].astype(F32) + rf[1, peer].astype(F32)
-            ss[pl.ds(peer, 1), :] = rs[peer]
-        return carry
-
-    lax.fori_loop(0, SEQ // 8, per_peer, 0)
-    for b in range(WIDTH // ROWS):
-        cols = slice(b * ROWS, (b + 1) * ROWS)
-        gain = skip[:, cols]
-        key, value = bk[:, cols].astype(F32), bv[:, cols].astype(F32)
-        grad = bg[:, cols].astype(F32)
-        source = (fk[:, cols].astype(F32) * fv[:, cols].astype(F32)).astype(BF16).astype(F32)
-        second = (key * value).astype(BF16).astype(F32)
-        upstream = (grad * bq[:, cols].astype(F32)).astype(BF16).astype(F32)
-        out[:, cols] = (fq[:, cols].astype(F32) * (xs[0, cols, :].T + gain * source)).astype(BF16)
-        gq[:, cols] = (grad * (xs[1, cols, :].T + gain * second)).astype(BF16)
-        through = xs[2, cols, :].T + gain * upstream
-        gk[:, cols] = (through * value).astype(BF16)
-        gv[:, cols] = (through * key).astype(BF16)
-    for b in range(QUARTER // ROWS):
-        cols = slice(b * ROWS, (b + 1) * ROWS)
-        gf[:, cols] = fs[cols, :].T
-    ss[...] = ss[...].T
-    even, odd = ss[pl.ds(0, 8, stride=2), :], ss[pl.ds(1, 8, stride=2), :]
-    lane = lax.broadcasted_iota(jnp.int32, (8, ROWS), 1)
-    gsk[...] = jnp.where(lane < SEQ, even, pltpu.roll(odd, SEQ, 1))
-
-
-def finish(r, rf, rs, fq, fk, fv, bq, bk, bv, bg, skip):
-    wide = jax.ShapeDtypeStruct((ROWS, WIDTH), BF16)
+    )(*values)
+
+
+def store_kernel(*refs):
+    count = len(refs) // 2
+    sems = refs[-1]
+    copies = [
+        pltpu.make_async_copy(refs[n], refs[count + n], sems.at[n]) for n in range(count)
+    ]
+    for copy in copies:
+        copy.start()
+    for copy in copies:
+        copy.wait()
+
+
+def store(values):
     return pl.pallas_call(
-        finish_kernel,
-        out_shape=(
-            wide,
-            wide,
-            wide,
-            wide,
-            jax.ShapeDtypeStruct((ROWS, QUARTER), F32),
-            jax.ShapeDtypeStruct((8, ROWS), F32),
-        ),
-        in_specs=[pl.BlockSpec(memory_space=pltpu.VMEM)] * 11,
-        out_specs=[pl.BlockSpec(memory_space=pltpu.VMEM)] * 6,
-        scratch_shapes=[
-            pltpu.VMEM((3, WIDTH, ROWS), F32),
-            pltpu.VMEM((QUARTER, ROWS), F32),
-            pltpu.VMEM((ROWS, ROWS), F32),
-        ],
-    )(r, rf, rs, fq, fk, fv, bq, bk, bv, bg, skip)
+        store_kernel,
+        out_shape=tuple(jax.ShapeDtypeStruct(v.shape, v.dtype) for v in values),
+        in_specs=[pl.BlockSpec(memory_space=pltpu.VMEM)] * len(values),
+        out_specs=[pl.BlockSpec(memory_space=pl.ANY)] * len(values),
+        scratch_shapes=[pltpu.SemaphoreType.DMA((len(values),))],
+    )(*[pltpu.with_memory_space_constraint(v, pltpu.VMEM) for v in values])
 
 
 def per_device(fwd_q, fwd_k, fwd_v, bwd_q, bwd_k, bwd_v, bwd_grad, filters, skip):
-    back, back_f, back_s = exchange(fwd_k, fwd_v, bwd_k, bwd_v, bwd_grad, bwd_q, filters)
-    *wide, skips = finish(
-        back, back_f, back_s, fwd_q, fwd_k, fwd_v, bwd_q, bwd_k, bwd_v, bwd_grad, skip[None, :]
+    done = exchange(
+        filters, bwd_k, bwd_v, bwd_grad, bwd_q, fwd_k, fwd_v, fwd_q, skip[None, :]
     )
+    *wide, skips = store(done)
     return (*wide, skips.reshape(WIDTH))
 
 

time: 65.8 us -> 59.1 us (0.90)
  Pallas kernels: 65 us -> 58.3 us
    pallas_call x2, Pallas kernels: 65 us -> 58.3 us  [the longest x1 57.3 us: exchange(): pl.pallas_call(main_kernel, out_shape=(wide, wide, wide, wide, pltpu.VMEM...]
where the time goes in v3:
time: 59.1 us; the launch traced here: 59 us
  Pallas kernels  58.3 us (99%)
  between operations  0.64 us (1%)
    pallas_call x1, Pallas kernels, exchange(): pl.pallas_call(main_kernel, out_shape=(wide, wide, wide, wide, pltpu.VMEM...  57.3 us

profile of v3, /device:TPU:1, one launch (start us, length us, event | category | flops | bytes accessed | tf_op | source)
XLA Modules:
  0.0 59.0 jit_solution(6448108324192756722)
XLA Ops:
  0.6 57.3 %shard_map.181 = (bf16[128,1024]{1,0:T(8,128)(2,1)S(1)}, bf16[128,1024]{1,0:T(8,128)(2,1)S(1)}, bf16[128,1024]{1,0:T(8,128)(2,1)S(1)}, bf16[128,1024]{1,0:T(8,12...) custom-call(f32[128,256]{1,0:T(8,128)} %refs_0_.1, bf16[128,1024]{1,0:T(8,128)(2,1)} %refs_1_.1, ...), custom_call_target="tpu_custom_call" | custom-call | tf_op jit(solution)/shard_map/pallas_call | solution.py:433
  57.9 1.1 %shard_map.182 = (bf16[128,1024]{1,0:T(8,128)(2,1)}, bf16[128,1024]{1,0:T(8,128)(2,1)}, bf16[128,1024]{1,0:T(8,128)(2,1)}, bf16[128,1024]{1,0:T(8,128)(2,1)}, f32[128,256]{1,0:T(8,128)}, /*index=5*/f32[8,128]{1,0:T(8,128)}) custom-call(bf16[128,1024]{1,0:T(8,128)(2,1)S(1)} %get-tuple-element.18.refs_0_, bf16[128,1024]{1,0:T(8,128)(2,1)S(1)} %get-tuple-element.19.refs_1_, ...), custom_call_target="tpu_custom_call" | custom-call | tf_op jit(solution)/shard_map/pallas_call | solution.py:484

commit v4 on v3

--- a/solution.py
+++ b/solution.py
@@ -138,6 +138,17 @@
         body(x * 16 + z * 4 + y_other)
 
 
+def every_peer_flat(me, body, itself=False):
+    x, z, y = me // 16, (me // 4) % 4, me % 4
+    xs = [((x + d) % 4) * 16 for d in (2, 1, 3, 0)]
+    ys = [(y + d) % 4 for d in (2, 1, 3, 0)]
+    for n, other in enumerate((3 - z, (z + 2) % 4, z + 1 - 2 * (z % 2), z)):
+        for a in range(4):
+            for b in range(4):
+                if itself or (n, a, b) != (3, 3, 3):
+                    body(xs[a] + other * 4 + ys[b])
+
+
 def push(src, dst, sems, target):
     copy = pltpu.make_async_remote_copy(
         src_ref=src,
@@ -156,7 +167,7 @@
     copied, loaded = refs[COPIED + 6 : 2 * COPIED + 6], refs[2 * COPIED + 6]
     (
         r, rf, rs, send, send_f, recv, filt, xs, fs, ss, spectra, y, terms, near_in, out_f, gs,
-        sent, got,
+        sent, got, ready,
     ) = refs[2 * COPIED + 7 :]
     fl, bk, bv, bg, bq, fk, fv, lead, trail, twist, ahead, back, fq, skip = copied
     me, group = lax.axis_index("seq"), lax.axis_index("chan")
@@ -169,14 +180,18 @@
     for load in loads:
         load.start()
 
-    def hello(seq, chan):
+    def hello(seq, chan, sem=barrier):
         pl.semaphore_signal(
-            barrier, inc=1, device_id={"seq": seq, "chan": chan}, device_id_type=MESH
+            sem, inc=1, device_id={"seq": seq, "chan": chan}, device_id_type=MESH
         )
 
-    every_peer(me, lambda peer: hello(peer, across), True)
-    every_peer(me, lambda peer: hello(peer, group))
+    every_peer_flat(me, lambda peer: hello(peer, group))
     hello(me, beside)
+
+    @pl.when(half == 0)
+    def _():
+        every_peer_flat(me, lambda peer: hello(peer, across), True)
+
 
     def sems(n):
         return sent.at[n], got.at[n]
@@ -240,19 +255,33 @@
     loads[1].wait()
     loads[2].wait()
     pack(1, bk, bv)
-    pl.semaphore_wait(barrier, 2 * SEQ)
+    pl.semaphore_wait(barrier, SEQ + SEQ * half)
     landing = filt.at[group, me]
+
+    def filters_across():
+        every_peer(
+            me,
+            lambda peer: push(send_f.at[peer], landing, sems(7), {"seq": peer, "chan": across}),
+            True,
+        )
+
+    @pl.when(half == 1)
+    def _():
+        every_peer_flat(me, lambda peer: hello(peer, across, ready), True)
+        filters_across()
+
     every_peer(me, lambda peer: push(send_f.at[peer], landing, sems(6), {"seq": peer}))
-    every_peer(
-        me,
-        lambda peer: push(send_f.at[peer], landing, sems(7), {"seq": peer, "chan": across}),
-        True,
-    )
     filt[group, me] = send_f[me]
     send_signal(1)
     loads[3].wait()
     loads[4].wait()
     pack(2, bg, bq)
+
+    @pl.when(half == 0)
+    def _():
+        pl.semaphore_wait(ready, SEQ)
+        filters_across()
+
     send_signal(2)
     loads[5].wait()
     loads[6].wait()
@@ -260,12 +289,11 @@
     send_signal(0)
     for load in loads[7:]:
         load.wait()
-    waiting(most(filt.at[group]), 6).wait_recv()
-    waiting(filt.at[across], 7).wait_recv()
-    moved = [
-        push(filt.at[group], filt.at[group], sems(8), {"chan": beside}),
-        push(filt.at[across], filt.at[across], sems(9), {"chan": beside}),
-    ]
+    moved = []
+    for held, landed in ((most(filt.at[group]), 6), (filt.at[across], 7)):
+        waiting(held, landed).wait_recv()
+        whole = filt.at[group if landed == 6 else across]
+        moved.append(push(whole, whole, sems(landed + 2), {"chan": beside}))
     for copy in moved:
         copy.wait_recv()
 
@@ -319,13 +347,10 @@
         spec = forward(cols, lead, twist, ahead)
         pairs = []
         for k in range(PART):
-            pairs.append(conj_times(pair_of(spectra[1, q * PART + k]), pair_of(spec[k])))
-        for k in range(PART):
+            spectra[2, q * PART + k] = spec[k]
             pairs.append(conj_times(pair_of(spectra[0, q * PART + k]), pair_of(spec[k])))
-        values = inverse(pairs, trail, twist, back)
-        for k in range(PART):
-            put(2, q * PART + k, values[k])
-            fs[q, pl.ds(k, SEQ, stride=PART), :] = values[PART + k]
+        for k, value in enumerate(inverse(pairs, trail, twist, back)):
+            fs[q, pl.ds(k, SEQ, stride=PART), :] = value
         return carry
 
     lax.fori_loop(0, GROUPS, correlate, 0)
@@ -335,7 +360,17 @@
         push(terms.at[2 * h + (1 - core)], near_in.at[h], sems(10 + h), {"chan": beside})
         for h in range(2)
     ]
-    send_back(2)
+
+    def through_of(q, carry):
+        pairs = []
+        for k in range(PART):
+            j = q * PART + k
+            pairs.append(conj_times(pair_of(spectra[1, j]), pair_of(spectra[2, j])))
+        for k, value in enumerate(inverse(pairs, trail, twist, back)):
+            put(2, q * PART + k, value)
+        return carry
+
+    lax.fori_loop(0, GROUPS, through_of, 0)
     for copy in swapped:
         copy.wait_recv()
     fs[0] = terms[group].astype(F32) + near_in[half].astype(F32)
@@ -351,7 +386,6 @@
         push(out_f.at[0, peer], rf.at[0, me], sems(12), {"seq": peer})
         push(gs, rs.at[me], sems(14), {"seq": peer})
 
-    every_peer(me, own_terms)
     every_peer(
         me,
         lambda peer: push(
@@ -359,8 +393,10 @@
         ),
         True,
     )
+    every_peer(me, own_terms)
     rf[0, me] = out_f[0, me]
     rs[me] = gs[...]
+    send_back(2)
 
     widen(0)
 
@@ -455,7 +491,7 @@
             pltpu.VMEM((4, WIDTH, ROWS), F32),
             pltpu.VMEM((GROUPS, QUARTER, ROWS), F32),
             pltpu.VMEM((ROWS, ROWS), F32),
-            pltpu.VMEM((2, HELD, SEQ, 2 * ROWS), F32),
+            pltpu.VMEM((3, HELD, SEQ, 2 * ROWS), F32),
             pltpu.VMEM((3, SEQ, HELD, ROWS), BF16),
             pltpu.VMEM((GROUPS, QUARTER, ROWS), BF16),
             pltpu.VMEM((2, QUARTER, ROWS), BF16),
@@ -463,6 +499,7 @@
             pltpu.VMEM((1, ROWS), F32),
             pltpu.SemaphoreType.DMA((15,)),
             pltpu.SemaphoreType.DMA((15,)),
+            pltpu.SemaphoreType.REGULAR,
         ],
         compiler_params=pltpu.CompilerParams(collective_id=0, has_side_effects=True),
     )(*values)

time: 59.1 us -> 57.2 us (0.968); the launches traced: 59 us -> 56.3 us
  Pallas kernels: 58.3 us -> 55.6 us
    pallas_call x1, Pallas kernels: 57.3 us -> 54.6 us  [exchange(): pl.pallas_call(main_kernel, out_shape=(wide, wide, wide, wide, pltpu.VMEM...]
where the time goes in v4:
time: 57.2 us; the launch traced here: 56.3 us
  Pallas kernels  55.6 us (97%)
  between operations  0.64 us (1%)
    pallas_call x1, Pallas kernels, exchange(): pl.pallas_call(main_kernel, out_shape=(wide, wide, wide, wide, pltpu.VMEM...  54.6 us

profile of v4, /device:TPU:1, one launch (start us, length us, event | category | flops | bytes accessed | tf_op | source)
XLA Modules:
  0.0 56.3 jit_solution(5139115395402261091)
XLA Ops:
  0.6 54.6 %shard_map.181 = (bf16[128,1024]{1,0:T(8,128)(2,1)S(1)}, bf16[128,1024]{1,0:T(8,128)(2,1)S(1)}, bf16[128,1024]{1,0:T(8,128)(2,1)S(1)}, bf16[128,1024]{1,0:T(8,12...) custom-call(f32[128,256]{1,0:T(8,128)} %refs_0_.1, bf16[128,1024]{1,0:T(8,128)(2,1)} %refs_1_.1, ...), custom_call_target="tpu_custom_call" | custom-call | tf_op jit(solution)/shard_map/pallas_call | solution.py:469
  55.2 1.1 %shard_map.182 = (bf16[128,1024]{1,0:T(8,128)(2,1)}, bf16[128,1024]{1,0:T(8,128)(2,1)}, bf16[128,1024]{1,0:T(8,128)(2,1)}, bf16[128,1024]{1,0:T(8,128)(2,1)}, f32[128,256]{1,0:T(8,128)}, /*index=5*/f32[8,128]{1,0:T(8,128)}) custom-call(bf16[128,1024]{1,0:T(8,128)(2,1)S(1)} %get-tuple-element.18.refs_0_, bf16[128,1024]{1,0:T(8,128)(2,1)S(1)} %get-tuple-element.19.refs_1_, ...), custom_call_target="tpu_custom_call" | custom-call | tf_op jit(solution)/shard_map/pallas_call | solution.py:521

commit v5 on v4

--- a/solution.py
+++ b/solution.py
@@ -20,6 +20,7 @@
 TOTAL = ROWS * SEQ
 WIDTH = SEQ * HELD
 QUARTER = SEQ * PART
+UNROLL = 2
 COPIED = 14
 DATA_LOW = True
 TABLE_LOW = True
@@ -116,37 +117,37 @@
     lax.fori_loop(0, SEQ // 8, step, 0)
 
 
-def every_peer(me, body, itself=False):
+def owner(seq, half):
+    x, z, y = seq // 16, (seq // 4) % 4, seq % 4
+    return x * 16 + (z + half * (3 - 2 * z)) * 4 + y
+
+
+def every_peer(me, half, body, flat=False):
     x, z, y = me // 16, (me // 4) % 4, me % 4
     ys = [(y + d) % 4 for d in (2, 1, 3, 0)]
+
+    def row(dx, other, count):
+        base = ((x + dx) % 4) * 16
+        owned = other + half * (3 - 2 * other)
+        for y_other in ys[:count]:
+            body(base + other * 4 + y_other, base + owned * 4 + y_other)
+
+    def rows(other, first):
+        if flat:
+            for dx in range(first, 4):
+                row(dx, other, 4)
+            return
+
+        def one(dx, carry):
+            row(dx, other, 4)
+            return carry
+
+        lax.fori_loop(first, 4, one, 0)
+
     for other in (3 - z, (z + 2) % 4, z + 1 - 2 * (z % 2)):
-
-        def plane(dx, carry, other=other):
-            for y_other in ys:
-                body(((x + dx) % 4) * 16 + other * 4 + y_other)
-            return carry
-
-        lax.fori_loop(0, 4, plane, 0)
-
-    def level(dx, carry):
-        for y_other in ys:
-            body(((x + dx) % 4) * 16 + z * 4 + y_other)
-        return carry
-
-    lax.fori_loop(1, 4, level, 0)
-    for y_other in ys if itself else ys[:3]:
-        body(x * 16 + z * 4 + y_other)
-
-
-def every_peer_flat(me, body, itself=False):
-    x, z, y = me // 16, (me // 4) % 4, me % 4
-    xs = [((x + d) % 4) * 16 for d in (2, 1, 3, 0)]
-    ys = [(y + d) % 4 for d in (2, 1, 3, 0)]
-    for n, other in enumerate((3 - z, (z + 2) % 4, z + 1 - 2 * (z % 2), z)):
-        for a in range(4):
-            for b in range(4):
-                if itself or (n, a, b) != (3, 3, 3):
-                    body(xs[a] + other * 4 + ys[b])
+        rows(other, 0)
+    rows(z, 1)
+    row(0, z, 3)
 
 
 def push(src, dst, sems, target):
@@ -166,13 +167,16 @@
     sources, (out, gq, gk, gv, gf, gsk) = refs[:COPIED], refs[COPIED : COPIED + 6]
     copied, loaded = refs[COPIED + 6 : 2 * COPIED + 6], refs[2 * COPIED + 6]
     (
-        r, rf, rs, send, send_f, recv, filt, xs, fs, ss, spectra, y, terms, near_in, out_f, gs,
-        sent, got, ready,
+        r, rf, rs, send, send_f, recv, filt, xs, fs, ss, spectra, y, terms, near_in, far_out,
+        far_in, out_f, gs, gs_line, sent, got, ready,
     ) = refs[2 * COPIED + 7 :]
     fl, bk, bv, bg, bq, fk, fv, lead, trail, twist, ahead, back, fq, skip = copied
     me, group = lax.axis_index("seq"), lax.axis_index("chan")
     core, half = group % 2, group // 2
     beside, across = 2 * half + (1 - core), 2 * (1 - half) + core
+    me_x, me_z, me_y = me // 16, (me // 4) % 4, me % 4
+    mirror = {"seq": me_x * 16 + (3 - me_z) * 4 + me_y, "chan": across}
+    mine = owner(me, half)
     barrier = pltpu.get_barrier_semaphore()
     loads = [
         pltpu.make_async_copy(sources[n], copied[n], loaded.at[n]) for n in range(COPIED)
@@ -180,18 +184,15 @@
     for load in loads:
         load.start()
 
-    def hello(seq, chan, sem=barrier):
-        pl.semaphore_signal(
-            sem, inc=1, device_id={"seq": seq, "chan": chan}, device_id_type=MESH
-        )
-
-    every_peer_flat(me, lambda peer: hello(peer, group))
-    hello(me, beside)
+    def hello(target, sem=barrier):
+        pl.semaphore_signal(sem, inc=1, device_id=target, device_id_type=MESH)
+
+    every_peer(me, half, lambda peer, _: hello({"seq": peer}), True)
+    hello({"chan": beside})
 
     @pl.when(half == 0)
     def _():
-        every_peer_flat(me, lambda peer: hello(peer, across), True)
-
+        hello(mirror)
 
     def sems(n):
         return sent.at[n], got.at[n]
@@ -221,9 +222,11 @@
 
     def send_signal(m):
         every_peer(
-            me, lambda peer: push(send.at[m, peer], recv.at[m, me], sems(m), {"seq": peer})
+            me,
+            half,
+            lambda peer, own: push(send.at[m, own], recv.at[m, me], sems(m), {"seq": peer}),
         )
-        recv[m, me] = send[m, me]
+        recv[m, me] = send[m, mine]
 
     def widen(m):
         waiting(most(recv.at[m]), m).wait_recv()
@@ -233,15 +236,17 @@
 
         in_steps(one)
 
-    def send_back(m):
+    def send_back(m, held):
         def one(s):
-            y[m, s] = xs[m, rows_of(s, HELD), :].astype(BF16)
+            y[m, s] = xs[held, rows_of(s, HELD), :].astype(BF16)
 
         in_steps(one)
         every_peer(
-            me, lambda peer: push(y.at[m, peer], r.at[m, me], sems(3 + m), {"seq": peer})
+            me,
+            half,
+            lambda peer, _: push(y.at[m, peer], r.at[m, mine], sems(3 + m), {"seq": peer}),
         )
-        r[m, me] = y[m, me]
+        r[m, mine] = y[m, me]
 
     loads[0].wait()
     for b in range(QUARTER // ROWS):
@@ -255,54 +260,47 @@
     loads[1].wait()
     loads[2].wait()
     pack(1, bk, bv)
-    pl.semaphore_wait(barrier, SEQ + SEQ * half)
-    landing = filt.at[group, me]
-
-    def filters_across():
-        every_peer(
-            me,
-            lambda peer: push(send_f.at[peer], landing, sems(7), {"seq": peer, "chan": across}),
-            True,
-        )
+
+    def pack_loaded(m, left, right, n):
+        loads[n].wait()
+        loads[n + 1].wait()
+        pack(m, left, right)
+
+    pl.semaphore_wait(barrier, SEQ + half)
 
     @pl.when(half == 1)
     def _():
-        every_peer_flat(me, lambda peer: hello(peer, across, ready), True)
-        filters_across()
-
-    every_peer(me, lambda peer: push(send_f.at[peer], landing, sems(6), {"seq": peer}))
-    filt[group, me] = send_f[me]
+        hello(mirror, ready)
+
+    every_peer(
+        me,
+        half,
+        lambda peer, own: push(send_f.at[own], filt.at[group, me], sems(6), {"seq": peer}),
+    )
+    filt[group, me] = send_f[mine]
     send_signal(1)
-    loads[3].wait()
-    loads[4].wait()
-    pack(2, bg, bq)
+    pack_loaded(2, bg, bq, 3)
+    send_signal(2)
+    pack_loaded(0, fk, fv, 5)
 
     @pl.when(half == 0)
     def _():
-        pl.semaphore_wait(ready, SEQ)
-        filters_across()
-
-    send_signal(2)
-    loads[5].wait()
-    loads[6].wait()
-    pack(0, fk, fv)
+        pl.semaphore_wait(ready, 1)
+
+    waiting(most(filt.at[group]), 6).wait_recv()
+    whole = filt.at[group]
+    moved = [push(whole, whole, sems(7), mirror), push(whole, whole, sems(8), {"chan": beside})]
     send_signal(0)
     for load in loads[7:]:
         load.wait()
-    moved = []
-    for held, landed in ((most(filt.at[group]), 6), (filt.at[across], 7)):
-        waiting(held, landed).wait_recv()
-        whole = filt.at[group if landed == 6 else across]
-        moved.append(push(whole, whole, sems(landed + 2), {"chan": beside}))
-    for copy in moved:
-        copy.wait_recv()
+    moved[0].wait_recv()
+    whole = filt.at[across]
+    moved.append(push(whole, whole, sems(9), {"chan": beside}))
 
     def filter_wide(s):
         for q in range(GROUPS):
             fs[q, pl.ds(s * PART, PART), :] = filt[q, s].astype(F32)
 
-    in_steps(filter_wide)
-
     def column(m, j):
         return xs[m, pl.ds(j, SEQ, stride=HELD), :]
 
@@ -311,27 +309,29 @@
 
     widen(1)
 
+    def second_ahead(q, carry):
+        cols = [column(1, q * PART + k) for k in range(PART)]
+        for k, spec in enumerate(forward(cols, lead, twist, ahead)):
+            spectra[0, q * PART + k] = spec
+        return carry
+
+    lax.fori_loop(0, GROUPS, second_ahead, 0, unroll=UNROLL)
+    for copy in moved[1:]:
+        copy.wait_recv()
+    in_steps(filter_wide)
+
     def second(q, carry):
-        cols = [column(1, q * PART + k) for k in range(PART)]
-        cols += [fs[q, pl.ds(k, SEQ, stride=PART), :] for k in range(PART)]
-        spec = forward(cols, lead, twist, ahead)
+        cols = [fs[q, pl.ds(k, SEQ, stride=PART), :] for k in range(PART)]
         pairs = []
-        for k in range(PART):
-            spectra[0, q * PART + k] = spec[k]
-            spectra[1, q * PART + k] = spec[PART + k]
-            pairs.append(times(pair_of(spec[PART + k]), pair_of(spec[k])))
+        for k, spec in enumerate(forward(cols, lead, twist, ahead)):
+            spectra[1, q * PART + k] = spec
+            pairs.append(times(pair_of(spec), pair_of(spectra[0, q * PART + k])))
         for k, value in enumerate(inverse(pairs, trail, twist, back)):
             put(3, q * PART + k, value)
         return carry
 
-    lax.fori_loop(0, GROUPS, second, 0)
-
-    def second_out(s):
-        y[1, s] = xs[3, rows_of(s, HELD), :].astype(BF16)
-
-    in_steps(second_out)
-    every_peer(me, lambda peer: push(y.at[1, peer], r.at[1, me], sems(4), {"seq": peer}))
-    r[1, me] = y[1, me]
+    lax.fori_loop(0, GROUPS, second, 0, unroll=UNROLL)
+    send_back(1, 3)
 
     widen(2)
     gs[...] = jnp.zeros_like(gs)
@@ -353,7 +353,7 @@
             fs[q, pl.ds(k, SEQ, stride=PART), :] = value
         return carry
 
-    lax.fori_loop(0, GROUPS, correlate, 0)
+    lax.fori_loop(0, GROUPS, correlate, 0, unroll=UNROLL)
     for q in range(GROUPS):
         terms[q] = (fs[q] * scale).astype(BF16)
     swapped = [
@@ -370,33 +370,18 @@
             put(2, q * PART + k, value)
         return carry
 
-    lax.fori_loop(0, GROUPS, through_of, 0)
+    lax.fori_loop(0, GROUPS, through_of, 0, unroll=UNROLL)
     for copy in swapped:
         copy.wait_recv()
+    far_out[...] = (terms[across].astype(F32) + near_in[1 - half].astype(F32)).astype(BF16)
+    far = push(far_out, far_in, sems(13), mirror)
+    line = [
+        push(gs, gs_line.at[mine // 4 % 4], sems(14), {"seq": me_x * 16 + other * 4 + me_y})
+        for other in (3 - me_z, (me_z + 2) % 4, me_z + 1 - 2 * (me_z % 2))
+    ]
+    gs_line[mine // 4 % 4] = gs[...]
     fs[0] = terms[group].astype(F32) + near_in[half].astype(F32)
-    fs[1] = terms[across].astype(F32) + near_in[1 - half].astype(F32)
-
-    def cut(s):
-        for n in range(2):
-            out_f[n, s] = fs[n, pl.ds(s * PART, PART), :].astype(BF16)
-
-    in_steps(cut)
-
-    def own_terms(peer):
-        push(out_f.at[0, peer], rf.at[0, me], sems(12), {"seq": peer})
-        push(gs, rs.at[me], sems(14), {"seq": peer})
-
-    every_peer(
-        me,
-        lambda peer: push(
-            out_f.at[1, peer], rf.at[1, me], sems(13), {"seq": peer, "chan": across}
-        ),
-        True,
-    )
-    every_peer(me, own_terms)
-    rf[0, me] = out_f[0, me]
-    rs[me] = gs[...]
-    send_back(2)
+    send_back(2, 2)
 
     widen(0)
 
@@ -410,8 +395,35 @@
             put(0, q * PART + k, value)
         return carry
 
-    lax.fori_loop(0, GROUPS, first, 0)
-    send_back(0)
+    lax.fori_loop(0, GROUPS, first, 0, unroll=UNROLL)
+    far.wait_recv()
+    fs[0] += far_in[...].astype(F32)
+
+    def cut(s):
+        out_f[s] = fs[0, pl.ds(s * PART, PART), :].astype(BF16)
+
+    in_steps(cut)
+    every_peer(
+        me,
+        half,
+        lambda peer, _: push(out_f.at[peer], rf.at[mine], sems(12), {"seq": peer}),
+    )
+    rf[mine] = out_f[me]
+    whole_line = waiting(gs_line.at[pl.ds(0, 3)], 14)
+    whole_line.wait_recv()
+
+    def plane(dx, carry):
+        for d in range(4):
+            peer = ((me_x + dx) % 4) * 16 + me_z * 4 + (me_y + d) % 4
+            push(gs_line, rs.at[me_x * 4 + me_y], sems(15), {"seq": peer})
+        return carry
+
+    lax.fori_loop(1, 4, plane, 0)
+    for d in range(1, 4):
+        peer = me_x * 16 + me_z * 4 + (me_y + d) % 4
+        push(gs_line, rs.at[me_x * 4 + me_y], sems(15), {"seq": peer})
+    rs[me_x * 4 + me_y] = gs_line[...]
+    send_back(0, 0)
 
     def unpack(m):
         waiting(most(r.at[m]), 3 + m).wait_recv()
@@ -434,16 +446,17 @@
         through = xs[2, cols, :].T + skip[:, cols] * product(bg[:, cols], bq[:, cols])
         gk[:, cols] = (through * bv[:, cols].astype(F32)).astype(BF16)
         gv[:, cols] = (through * bk[:, cols].astype(F32)).astype(BF16)
-    last = [waiting(most(rf.at[0]), 12), waiting(rf.at[1], 13), waiting(most(rs), 14)]
+    last = [waiting(most(rf), 12), waiting(rs.at[pl.ds(0, 15)], 15)]
     for copy in last:
         copy.wait_recv()
     ss[...] = jnp.zeros_like(ss)
 
-    def unpack_terms(peer):
-        fs[0, pl.ds(peer, PART, stride=SEQ), :] = rf[0, peer].astype(F32) + rf[1, peer].astype(F32)
-        ss[pl.ds(peer, 1), :] = rs[peer]
+    def unpack_terms(p):
+        fs[0, pl.ds(p, PART, stride=SEQ), :] = rf[p].astype(F32)
 
     in_steps(unpack_terms)
+    for p in range(SEQ):
+        ss[p : p + 1, :] = rs[(p // 16) * 4 + p % 4, (p // 4) % 4]
     for cols in blocks[: QUARTER // ROWS]:
         gf[:, cols] = fs[0, cols, :].T
     ss[...] = ss[...].T
@@ -458,8 +471,7 @@
         waiting(most(send.at[m]), m).wait_send()
         waiting(most(r.at[m]), 3 + m).wait_send()
     waiting(most(send_f), 6).wait_send()
-    waiting(send_f, 7).wait_send()
-    for copy in moved + swapped + last:
+    for copy in [*moved, *swapped, far, whole_line, *last]:
         copy.wait_send()
 
 
@@ -482,8 +494,8 @@
             *[pltpu.VMEM(v.shape, v.dtype) for v in values],
             pltpu.SemaphoreType.DMA((COPIED,)),
             pltpu.VMEM((3, SEQ, HELD, ROWS), BF16),
-            pltpu.VMEM((2, SEQ, PART, ROWS), BF16),
-            pltpu.VMEM((SEQ, 1, ROWS), F32),
+            pltpu.VMEM((SEQ, PART, ROWS), BF16),
+            pltpu.VMEM((16, 4, 1, ROWS), F32),
             pltpu.VMEM((3, SEQ, HELD, ROWS), BF16),
             pltpu.VMEM((SEQ, PART, ROWS), BF16),
             pltpu.VMEM((3, SEQ, HELD, ROWS), BF16),
@@ -495,10 +507,13 @@
             pltpu.VMEM((3, SEQ, HELD, ROWS), BF16),
             pltpu.VMEM((GROUPS, QUARTER, ROWS), BF16),
             pltpu.VMEM((2, QUARTER, ROWS), BF16),
-            pltpu.VMEM((2, SEQ, PART, ROWS), BF16),
+            pltpu.VMEM((QUARTER, ROWS), BF16),
+            pltpu.VMEM((QUARTER, ROWS), BF16),
+            pltpu.VMEM((SEQ, PART, ROWS), BF16),
             pltpu.VMEM((1, ROWS), F32),
-            pltpu.SemaphoreType.DMA((15,)),
-            pltpu.SemaphoreType.DMA((15,)),
+            pltpu.VMEM((4, 1, ROWS), F32),
+            pltpu.SemaphoreType.DMA((16,)),
+            pltpu.SemaphoreType.DMA((16,)),
             pltpu.SemaphoreType.REGULAR,
         ],
         compiler_params=pltpu.CompilerParams(collective_id=0, has_side_effects=True),

time: 57.2 us -> 55.1 us (0.963); the launches traced: 56.3 us -> 55 us
  Pallas kernels: 55.6 us -> 54.4 us
    pallas_call x1, Pallas kernels: 54.6 us -> 53.3 us  [exchange(): pl.pallas_call(main_kernel, out_shape=(wide, wide, wide, wide, pltpu.VMEM...]
where the time goes in v5:
time: 55.1 us; the launch traced here: 55 us
  Pallas kernels  54.4 us (99%)
  between operations  0.64 us (1%)
    pallas_call x1, Pallas kernels, exchange(): pl.pallas_call(main_kernel, out_shape=(wide, wide, wide, wide, pltpu.VMEM...  53.3 us

profile of v5, /device:TPU:1, one launch (start us, length us, event | category | flops | bytes accessed | tf_op | source)
XLA Modules:
  0.0 55.0 jit_solution(10513383826153143433)
XLA Ops:
  0.6 53.3 %shard_map.181 = (bf16[128,1024]{1,0:T(8,128)(2,1)S(1)}, bf16[128,1024]{1,0:T(8,128)(2,1)S(1)}, bf16[128,1024]{1,0:T(8,128)(2,1)S(1)}, bf16[128,1024]{1,0:T(8,12...) custom-call(f32[128,256]{1,0:T(8,128)} %refs_0_.1, bf16[128,1024]{1,0:T(8,128)(2,1)} %refs_1_.1, ...), custom_call_target="tpu_custom_call" | custom-call | tf_op jit(solution)/shard_map/pallas_call | solution.py:481
  54.0 1.1 %shard_map.182 = (bf16[128,1024]{1,0:T(8,128)(2,1)}, bf16[128,1024]{1,0:T(8,128)(2,1)}, bf16[128,1024]{1,0:T(8,128)(2,1)}, bf16[128,1024]{1,0:T(8,128)(2,1)}, f32[128,256]{1,0:T(8,128)}, /*index=5*/f32[8,128]{1,0:T(8,128)}) custom-call(bf16[128,1024]{1,0:T(8,128)(2,1)S(1)} %get-tuple-element.18.refs_0_, bf16[128,1024]{1,0:T(8,128)(2,1)S(1)} %get-tuple-element.19.refs_1_, ...), custom_call_target="tpu_custom_call" | custom-call | tf_op jit(solution)/shard_map/pallas_call | solution.py:536

commit v6 on v5

--- a/solution.py
+++ b/solution.py
@@ -22,7 +22,7 @@
 QUARTER = SEQ * PART
 UNROLL = 2
 COPIED = 14
-DATA_LOW = True
+DATA_LOW = False
 TABLE_LOW = True
 
 

time: 55.1 us -> 53 us (0.962)
  Pallas kernels: 54.4 us -> 52.2 us
    pallas_call x1, Pallas kernels: 53.3 us -> 51.2 us  [exchange(): pl.pallas_call(main_kernel, out_shape=(wide, wide, wide, wide, pltpu.VMEM...]
where the time goes in v6:
time: 53 us; the launch traced here: 52.9 us
  Pallas kernels  52.2 us (98%)
  between operations  0.64 us (1%)
    pallas_call x1, Pallas kernels, exchange(): pl.pallas_call(main_kernel, out_shape=(wide, wide, wide, wide, pltpu.VMEM...  51.2 us

profile of v6, /device:TPU:1, one launch (start us, length us, event | category | flops | bytes accessed | tf_op | source)
XLA Modules:
  0.0 52.9 jit_solution(5511046645696059463)
XLA Ops:
  0.6 51.2 %shard_map.181 = (bf16[128,1024]{1,0:T(8,128)(2,1)S(1)}, bf16[128,1024]{1,0:T(8,128)(2,1)S(1)}, bf16[128,1024]{1,0:T(8,128)(2,1)S(1)}, bf16[128,1024]{1,0:T(8,12...) custom-call(f32[128,256]{1,0:T(8,128)} %refs_0_.1, bf16[128,1024]{1,0:T(8,128)(2,1)} %refs_1_.1, ...), custom_call_target="tpu_custom_call" | custom-call | tf_op jit(solution)/shard_map/pallas_call | solution.py:481
  51.8 1.1 %shard_map.182 = (bf16[128,1024]{1,0:T(8,128)(2,1)}, bf16[128,1024]{1,0:T(8,128)(2,1)}, bf16[128,1024]{1,0:T(8,128)(2,1)}, bf16[128,1024]{1,0:T(8,128)(2,1)}, f32[128,256]{1,0:T(8,128)}, /*index=5*/f32[8,128]{1,0:T(8,128)}) custom-call(bf16[128,1024]{1,0:T(8,128)(2,1)S(1)} %get-tuple-element.18.refs_0_, bf16[128,1024]{1,0:T(8,128)(2,1)S(1)} %get-tuple-element.19.refs_1_, ...), custom_call_target="tpu_custom_call" | custom-call | tf_op jit(solution)/shard_map/pallas_call | solution.py:536

commit v7 on v6

--- a/solution.py
+++ b/solution.py
@@ -20,7 +20,7 @@
 TOTAL = ROWS * SEQ
 WIDTH = SEQ * HELD
 QUARTER = SEQ * PART
-UNROLL = 2
+UNROLL = 4
 COPIED = 14
 DATA_LOW = False
 TABLE_LOW = True
@@ -132,21 +132,20 @@
         for y_other in ys[:count]:
             body(base + other * 4 + y_other, base + owned * 4 + y_other)
 
-    def rows(other, first):
-        if flat:
-            for dx in range(first, 4):
-                row(dx, other, 4)
-            return
-
-        def one(dx, carry):
+    others = ((z + 2) % 4, z + 1 - 2 * (z % 2), 3 - z, z)
+
+    def plane(dx, carry):
+        for other in others:
             row(dx, other, 4)
-            return carry
-
-        lax.fori_loop(first, 4, one, 0)
-
-    for other in (3 - z, (z + 2) % 4, z + 1 - 2 * (z % 2)):
-        rows(other, 0)
-    rows(z, 1)
+        return carry
+
+    if flat:
+        for dx in range(1, 4):
+            plane(dx, 0)
+    else:
+        lax.fori_loop(1, 4, plane, 0)
+    for other in others[:3]:
+        row(0, other, 4)
     row(0, z, 3)
 
 

time: 53 us -> 51.5 us (0.972)
  Pallas kernels: 52.2 us -> 50.7 us
    pallas_call x1, Pallas kernels: 51.2 us -> 49.7 us  [exchange(): pl.pallas_call(main_kernel, out_shape=(wide, wide, wide, wide, pltpu.VMEM...]
where the time goes in v7:
time: 51.5 us; the launch traced here: 51.4 us
  Pallas kernels  50.7 us (98%)
  between operations  0.64 us (1%)
    pallas_call x1, Pallas kernels, exchange(): pl.pallas_call(main_kernel, out_shape=(wide, wide, wide, wide, pltpu.VMEM...  49.7 us
    pallas_call x1, Pallas kernels, store(): pl.pallas_call(store_kernel, out_shape=tuple((jax.ShapeDtypeStruct(v.shap...  1.06 us

profile of v7, /device:TPU:1, one launch (start us, length us, event | category | flops | bytes accessed | tf_op | source)
XLA Modules:
  0.0 51.4 jit_solution(6541903934825412951)
XLA Ops:
  0.6 49.7 %shard_map.181 = (bf16[128,1024]{1,0:T(8,128)(2,1)S(1)}, bf16[128,1024]{1,0:T(8,128)(2,1)S(1)}, bf16[128,1024]{1,0:T(8,128)(2,1)S(1)}, bf16[128,1024]{1,0:T(8,12...) custom-call(f32[128,256]{1,0:T(8,128)} %refs_0_.1, bf16[128,1024]{1,0:T(8,128)(2,1)} %refs_1_.1, ...), custom_call_target="tpu_custom_call" | custom-call | tf_op jit(solution)/shard_map/pallas_call | solution.py:480
  50.3 1.1 %shard_map.182 = (bf16[128,1024]{1,0:T(8,128)(2,1)}, bf16[128,1024]{1,0:T(8,128)(2,1)}, bf16[128,1024]{1,0:T(8,128)(2,1)}, bf16[128,1024]{1,0:T(8,128)(2,1)}, f32[128,256]{1,0:T(8,128)}, /*index=5*/f32[8,128]{1,0:T(8,128)}) custom-call(bf16[128,1024]{1,0:T(8,128)(2,1)S(1)} %get-tuple-element.18.refs_0_, bf16[128,1024]{1,0:T(8,128)(2,1)S(1)} %get-tuple-element.19.refs_1_, ...), custom_call_target="tpu_custom_call" | custom-call | tf_op jit(solution)/shard_map/pallas_call | solution.py:535

commit v8 on v7

--- a/solution.py
+++ b/solution.py
@@ -108,13 +108,13 @@
     return pl.ds(pl.multiple_of(s * count, count), count)
 
 
-def in_steps(body):
+def in_steps(body, flat=False):
     def step(n, carry):
         for k in range(8):
             body(n * 8 + k)
         return carry
 
-    lax.fori_loop(0, SEQ // 8, step, 0)
+    lax.fori_loop(0, SEQ // 8, step, 0, unroll=SEQ // 8 if flat else 1)
 
 
 def owner(seq, half):
@@ -424,13 +424,13 @@
     rs[me_x * 4 + me_y] = gs_line[...]
     send_back(0, 0)
 
-    def unpack(m):
+    def unpack(m, flat=False):
         waiting(most(r.at[m]), 3 + m).wait_recv()
 
         def one(peer):
             xs[m, pl.ds(peer, HELD, stride=SEQ), :] = r[m, peer].astype(F32)
 
-        in_steps(one)
+        in_steps(one, flat)
 
     def product(left, right):
         return (left.astype(F32) * right.astype(F32)).astype(BF16).astype(F32)
@@ -462,9 +462,11 @@
     even, odd = ss[pl.ds(0, 8, stride=2), :], ss[pl.ds(1, 8, stride=2), :]
     wide = lax.broadcasted_iota(jnp.int32, (8, ROWS), 1)
     gsk[...] = jnp.where(wide < SEQ, even, pltpu.roll(odd, SEQ, 1))
-    unpack(0)
     for cols in blocks:
-        mixed = xs[0, cols, :].T + skip[:, cols] * product(fk[:, cols], fv[:, cols])
+        xs[3, cols, :] = skip[:, cols] * product(fk[:, cols], fv[:, cols])
+    unpack(0, True)
+    for cols in blocks:
+        mixed = xs[0, cols, :].T + xs[3, cols, :]
         out[:, cols] = (fq[:, cols].astype(F32) * mixed).astype(BF16)
     for m in range(3):
         waiting(most(send.at[m]), m).wait_send()

time: 51.5 us -> 51.3 us (level)
  no operation moved by 1% of the time
where the time goes in v8:
time: 51.3 us; the launch traced here: 51.2 us
  Pallas kernels  50.6 us (99%)
  between operations  0.64 us (1%)
    pallas_call x1, Pallas kernels, exchange(): pl.pallas_call(main_kernel, out_shape=(wide, wide, wide, wide, pltpu.VMEM...  49.5 us
    pallas_call x1, Pallas kernels, store(): pl.pallas_call(store_kernel, out_shape=tuple((jax.ShapeDtypeStruct(v.shap...  1.06 us

profile of v8, /device:TPU:1, one launch (start us, length us, event | category | flops | bytes accessed | tf_op | source)
XLA Modules:
  0.0 51.2 jit_solution(17408581584086674244)
XLA Ops:
  0.6 49.5 %shard_map.181 = (bf16[128,1024]{1,0:T(8,128)(2,1)S(1)}, bf16[128,1024]{1,0:T(8,128)(2,1)S(1)}, bf16[128,1024]{1,0:T(8,128)(2,1)S(1)}, bf16[128,1024]{1,0:T(8,12...) custom-call(f32[128,256]{1,0:T(8,128)} %refs_0_.1, bf16[128,1024]{1,0:T(8,128)(2,1)} %refs_1_.1, ...), custom_call_target="tpu_custom_call" | custom-call | tf_op jit(solution)/shard_map/pallas_call | solution.py:482
  50.2 1.1 %shard_map.182 = (bf16[128,1024]{1,0:T(8,128)(2,1)}, bf16[128,1024]{1,0:T(8,128)(2,1)}, bf16[128,1024]{1,0:T(8,128)(2,1)}, bf16[128,1024]{1,0:T(8,128)(2,1)}, f32[128,256]{1,0:T(8,128)}, /*index=5*/f32[8,128]{1,0:T(8,128)}) custom-call(bf16[128,1024]{1,0:T(8,128)(2,1)S(1)} %get-tuple-element.18.refs_0_, bf16[128,1024]{1,0:T(8,128)(2,1)S(1)} %get-tuple-element.19.refs_1_, ...), custom_call_target="tpu_custom_call" | custom-call | tf_op jit(solution)/shard_map/pallas_call | solution.py:537
